TPU v7x, 256 devices: a whole 4x4x8 slice. The times are simulated.
256 devices in a mesh: dp: 16 (over x_lo, y, core), ctx: 16 (over x_hi, z).
Axes of the slice: x: 4 (x_hi: 2, x_lo: 2; x = x_hi * 2 + x_lo), y: 4, z: 8, core: 2. Of those that a mesh axis runs over, the one named last changes fastest.
Arguments:
- query: bfloat16 [16, 2048, 2048], P('dp', 'ctx'), may hold values from -16 to 16
- keys: bfloat16 [16, 2048, 2048], P('dp', 'ctx'), may hold values from -16 to 16
- values: bfloat16 [16, 2048, 2048], P('dp', 'ctx'), may hold values from -6 to 6
- codes: int32 [16, 2048, 4], P('dp', 'ctx'), may hold values from 0 to 2047
- w_in: bfloat16 [2048, 1024], replicated, may hold values from -0.125 to 0.125
- table: bfloat16 [2048, 1024], replicated, may hold values from -0.67 to 0.67
- gain: float32 [1024], replicated, may hold values from 0.5 to 1.5
- w_qkv: bfloat16 [1024, 1536], P('dp'), may hold values from -0.140625 to 0.140625
- w_out: bfloat16 [512, 1024], P('dp'), may hold values from -0.25 to 0.25
Outputs:
- grad_qkv: float32 [1024, 1536], P('dp')
- grad_out: float32 [512, 1024], P('dp')
All inputs are finite; a program needn't handle non-finite values.
Results may differ from a plain program's by a relative error of at most 0.01.
Values may be sent and summed in bfloat16 or wider, within the bound.
No kernel may reach another device: no remote copies, remote signals or barrier semaphores. Data moves between devices by JAX's collectives and lax.ppermute only.
A program may use at most 128 MiB of HBM per device.

v0:
```python
import functools
import math

import jax
import jax.numpy as jnp
from jax import lax
from jax.experimental import pallas as pl
from jax.experimental.pallas import tpu as pltpu
from jax.sharding import Mesh
from jax.sharding import PartitionSpec as P

HEAD_DIM = 128
DEPTH_HEAD = 64
DP = ("dp_0", "dp_1", "dp_2")
CTX = ("ctx_0", "ctx_1")
PLANE = ("dp_0", "dp_1", "ctx_0")

bf16, f32 = jnp.bfloat16, jnp.float32
NEG = -1e30
EPS = 1e-6
NT = (((1,), (1,)), ((), ()))


def dot(a, b):
    return jnp.dot(a, b, preferred_element_type=f32)


def dot_nt(a, b):
    return lax.dot_general(a, b, NT, preferred_element_type=f32)


def attend_body(x_ref, o_ref, *, step):
    blocks, _, rows, dim = x_ref.shape
    for i in range(0, blocks, step):
        seen = i + step
        q = x_ref[i:seen, 0].reshape(step * rows, dim)
        k = x_ref[0:seen, 1].reshape(seen * rows, dim)
        v = x_ref[0:seen, 2].reshape(seen * rows, dim)
        s = dot_nt(q, k) * (1.0 / math.sqrt(dim))
        shape = (step * rows, step * rows)
        ok = lax.broadcasted_iota(jnp.int32, shape, 1) <= lax.broadcasted_iota(jnp.int32, shape, 0)
        last = jnp.where(ok, s[:, i * rows :], NEG)
        s = last if i == 0 else jnp.concatenate([s[:, : i * rows], last], axis=1)
        p = jnp.exp(s - jnp.max(s, axis=1, keepdims=True))
        total = jnp.sum(p, axis=1, keepdims=True)
        out = dot(p.astype(bf16), v) / total
        o_ref[i:seen] = out.astype(bf16).reshape(step, rows, dim)


def embed_body(codes_ref, table_ref, o_ref, hot_ref):
    count, frames, width = o_ref.shape
    entries = table_ref.shape[0]
    ids = lax.broadcasted_iota(jnp.int32, (frames, entries), 1)
    for c in range(count):
        hot_ref[c * frames : (c + 1) * frames] = (
            (ids == codes_ref[:, c : c + 1]).astype(f32).astype(bf16)
        )
    tile = 256

    @pl.loop(0, width // tile)
    def _(j):
        cols = pl.ds(pl.multiple_of(j * tile, tile), tile)
        rows = dot(hot_ref[...], table_ref[:, cols])
        o_ref[:, :, cols] = rows.astype(bf16).reshape(count, frames, tile)


def put_split(ref, k, frames, count, term):
    high = term.astype(bf16)
    ref[k * frames : (k + 1) * frames] = high
    ref[(count + k) * frames : (count + k + 1) * frames] = (term - high.astype(f32)).astype(bf16)


def head_sums(ref, rows, heads_block, store):
    width = heads_block.shape[0]
    for j in range(ref.shape[1] // width):
        cols = slice(j * width, (j + 1) * width)
        store(cols, dot(ref[:rows, cols], heads_block) + dot(ref[rows:, cols], heads_block))


def same_head(width, head):
    r = lax.broadcasted_iota(jnp.int32, (width, width), 0) // head
    c = lax.broadcasted_iota(jnp.int32, (width, width), 1) // head
    return (r == c).astype(f32).astype(bf16)


def pairs_of(positions):
    return [(c, e) for c in range(positions) for e in range(c + 1)]


def depth_body(
    place_ref, att_ref, emb_ref, codes_ref, gain_ref, w_in_hbm, table_hbm, w0_hbm, w1_hbm, w2_hbm, w3_hbm,
    t0_hbm, t1_hbm, t2_hbm, t3_hbm, keep_ref, send_ref,
    w_in_ref, table_ref, w_ref, w_out_ref, x_ref, n_ref, n_t_ref, qkv_ref, term_ref, s_ref, p_ref, mix_ref, mix_t_ref, inv_ref,
    logit_ref, g_ref, dr_ref, dqkv_ref, stage_ref, sems, in_sems, table_sem,
    *, weight, head,
):
    frames, positions = codes_ref.shape
    width = x_ref.shape[1]
    entries = table_ref.shape[0]
    dh = w_out_ref.shape[0]
    owners, _, rows_qkv, _ = stage_ref.shape
    rows_out = rows_qkv // 2
    half = width // 2
    tile = 256
    side = place_ref[2]
    z_ref = x_ref
    dz_ref = logit_ref.at[:, :width]
    dmix_ref = logit_ref.at[:, width : width + dh]
    row = lambda c: pl.ds(c * frames, frames)

    tile_cols = lambda j: pl.ds(pl.multiple_of(j * tile, tile), tile)
    load_in = lambda j: pltpu.make_async_copy(
        w_in_hbm.at[:, tile_cols(j)], w_in_ref.at[:, tile_cols(j)], in_sems.at[j]
    )
    load_table = pltpu.make_async_copy(table_hbm, table_ref, table_sem)
    for j in range(width // tile):
        load_in(j).start()
    loads = []
    mine, twins = (w0_hbm, w1_hbm, w2_hbm, w3_hbm), (t0_hbm, t1_hbm, t2_hbm, t3_hbm)
    for twin, refs in enumerate((mine, twins)):
        for back, ref in enumerate(refs):
            for plane in range(2):
                at = (place_ref[0] + plane) % 2
                at = at * len(refs) + (place_ref[1] + len(refs) - back) % len(refs)
                at = at * 2 + (side + twin) % 2
                rows = pl.ds(pl.multiple_of(at * rows_qkv, rows_qkv), rows_qkv)
                loads.append(pltpu.make_async_copy(ref.at[plane], w_ref.at[rows], sems.at[len(loads)]))
                loads[-1].start()
    load_table.start()
    att = jnp.concatenate([att_ref[h] for h in range(att_ref.shape[0])], axis=1)

    @pl.loop(0, width // tile)
    def _(j):
        cols = pl.ds(pl.multiple_of(j * tile, tile), tile)
        load_in(j).wait()
        hidden = dot(att, w_in_ref[:, cols])
        x_ref[row(0), cols] = hidden
        for c in range(1, positions):
            x_ref[row(c), cols] = hidden + emb_ref[c - 1, :, cols].astype(f32)

    for c in range(positions):
        x = x_ref[row(c), :]
        scale = lax.rsqrt(jnp.mean(x * x, axis=1, keepdims=True) + EPS)
        normed = (x * scale * gain_ref[...]).astype(bf16)
        n_ref[row(c), :] = normed
        n_t_ref[:, row(c)] = normed.T

    for load in loads:
        load.wait()
    for d in range(2 * owners):
        for k in range(2):
            w_out_ref[d * rows_out : (d + 1) * rows_out, k * half : (k + 1) * half] = w_ref[
                d * rows_qkv + k * rows_out : d * rows_qkv + (k + 1) * rows_out, 3 * dh :
            ]

    @pl.loop(0, 3 * dh // tile)
    def _(j):
        cols = pl.ds(pl.multiple_of(j * tile, tile), tile)
        qkv_ref[:, cols] = dot(n_ref[...], w_ref[:, cols]).astype(bf16)

    block = same_head(tile, head)
    scale = 1.0 / math.sqrt(head)
    pairs = pairs_of(positions)
    part = lambda c, k: qkv_ref[row(c), k * dh : (k + 1) * dh].astype(f32)
    count = len(pairs)
    pair = lambda c, e: pl.ds(pairs.index((c, e)) * frames, frames)

    def store_scores(cols, values):
        s_ref[:, cols] = values * scale

    for k, (c, e) in enumerate(pairs):
        put_split(term_ref, k, frames, count, part(c, 0) * part(e, 1))
    head_sums(term_ref, count * frames, block, store_scores)
    for c in range(positions):
        scores = [s_ref[pair(c, e), :] for e in range(c + 1)]
        top = functools.reduce(jnp.maximum, scores)
        raised = [jnp.exp(s - top) for s in scores]
        fraction = 1.0 / functools.reduce(jnp.add, raised)
        mixed = jnp.zeros((frames, dh), f32)
        for e in range(c + 1):
            p = raised[e] * fraction
            p_ref[pair(c, e), :] = p
            mixed = mixed + p * part(e, 2)
        mixed = mixed.astype(bf16)
        mix_ref[row(c), :] = mixed
        mix_t_ref[:, row(c)] = mixed.T

    @pl.loop(0, width // tile)
    def _(j):
        cols = pl.ds(pl.multiple_of(j * tile, tile), tile)
        z_ref[:, cols] = x_ref[:, cols] + dot(mix_ref[...], w_out_ref[:, cols])

    for c in range(positions):
        r = z_ref[row(c), :]
        inv = lax.rsqrt(jnp.mean(r * r, axis=1, keepdims=True) + EPS)
        inv_ref[row(c), :] = jnp.broadcast_to(inv, (frames, inv_ref.shape[1]))
        z = r * inv
        z_ref[row(c), :] = z
        dr_ref[row(c), :] = z.astype(bf16)

    load_table.wait()

    @pl.loop(0, entries // tile)
    def _(j):
        cols = pl.ds(pl.multiple_of(j * tile, tile), tile)
        logit_ref[:, cols] = dot_nt(dr_ref[...], table_ref[cols, :])

    ids = lax.broadcasted_iota(jnp.int32, (frames, entries), 1)
    for c in range(positions):
        s = logit_ref[row(c), :]
        e = jnp.exp(s - jnp.max(s, axis=1, keepdims=True))
        total = jnp.sum(e, axis=1, keepdims=True)
        hit = jnp.where(ids == codes_ref[:, c : c + 1], weight, 0.0)
        g_ref[row(c), :] = (e * (weight / total) - hit).astype(bf16)

    @pl.loop(0, width // tile)
    def _(j):
        cols = pl.ds(pl.multiple_of(j * tile, tile), tile)
        dz_ref[:, cols] = dot(g_ref[...], table_ref[:, cols])

    for c in range(positions):
        dz, z = dz_ref[row(c), :], z_ref[row(c), :]
        along = jnp.mean(dz * z, axis=1, keepdims=True)
        dr_ref[row(c), :] = (inv_ref[row(c), 0:1] * (dz - z * along)).astype(bf16)

    for j in range(width // tile):
        part_out = dot(mix_t_ref[...], dr_ref[:, j * tile : (j + 1) * tile]).astype(bf16)
        stage_ref[:, :, 0:rows_out, :] = part_out.reshape(owners, 2, rows_out, tile)
        k, at = divmod(j * tile, half)
        rows = slice(k * rows_out, (k + 1) * rows_out)
        cols = slice(3 * dh + at, 3 * dh + at + tile)
        keep_ref[:, rows, cols] = stage_ref[:, side, 0:rows_out, :]
        send_ref[:, rows, cols] = stage_ref[:, 1 - side, 0:rows_out, :]

    @pl.loop(0, dh // tile)
    def _(j):
        cols = pl.ds(pl.multiple_of(j * tile, tile), tile)
        dmix_ref[:, cols] = dot_nt(dr_ref[...], w_out_ref[cols, :])

    def store_plain(cols, values):
        s_ref[:, cols] = values

    for k, (c, e) in enumerate(pairs):
        put_split(term_ref, k, frames, count, dmix_ref[row(c), :] * part(e, 2))
    head_sums(term_ref, count * frames, block, store_plain)
    dk = [jnp.zeros((frames, dh), f32) for _ in range(positions)]
    dv = [jnp.zeros((frames, dh), f32) for _ in range(positions)]
    for c in range(positions):
        dm = dmix_ref[row(c), :]
        probs = [p_ref[pair(c, e), :] for e in range(c + 1)]
        dprobs = [s_ref[pair(c, e), :] for e in range(c + 1)]
        along = functools.reduce(jnp.add, [d * p for d, p in zip(dprobs, probs)])
        q = part(c, 0)
        dq = jnp.zeros((frames, dh), f32)
        for e in range(c + 1):
            ds = probs[e] * (dprobs[e] - along) * scale
            dq = dq + ds * part(e, 1)
            dk[e] = dk[e] + ds * q
            dv[e] = dv[e] + probs[e] * dm
        dqkv_ref[row(c), 0:dh] = dq.astype(bf16)
    for c in range(positions):
        dqkv_ref[row(c), dh : 2 * dh] = dk[c].astype(bf16)
        dqkv_ref[row(c), 2 * dh :] = dv[c].astype(bf16)

    @pl.loop(0, 3 * dh // tile)
    def _(j):
        cols = pl.ds(pl.multiple_of(j * tile, tile), tile)
        part_qkv = dot(n_t_ref[...], dqkv_ref[:, cols]).astype(bf16)
        stage_ref[...] = part_qkv.reshape(owners, 2, rows_qkv, tile)
        keep_ref[:, :, cols] = stage_ref[:, side]
        send_ref[:, :, cols] = stage_ref[:, 1 - side]


def pack_body(query_ref, keys_ref, values_ref, o_ref):
    for d in range(o_ref.shape[0]):
        cols = slice(d * o_ref.shape[3], (d + 1) * o_ref.shape[3])
        for k, ref in enumerate((query_ref, keys_ref, values_ref)):
            o_ref[d, k] = ref[0, :, cols]


def add_cut_body(a_ref, b_ref, o_ref):
    width = o_ref.shape[3]
    for k in range(o_ref.shape[1]):
        cols = slice(k * width, (k + 1) * width)
        o_ref[:, k] = (a_ref[:, :, cols].astype(f32) + b_ref[:, :, cols].astype(f32)).astype(bf16)


def fold_cut_body(x_ref, o_ref):
    width = o_ref.shape[2]
    for j in range(o_ref.shape[0]):
        cols = slice(j * width, (j + 1) * width)
        o_ref[j] = functools.reduce(
            jnp.add, [x_ref[d, :, cols].astype(f32) for d in range(x_ref.shape[0])]
        ).astype(bf16)


def fold_copy_body(x_ref, o_ref):
    total = functools.reduce(jnp.add, [x_ref[d].astype(f32) for d in range(x_ref.shape[0])])
    for j in range(o_ref.shape[0]):
        o_ref[j] = total.astype(bf16)


def lay_out_body(x_ref, qkv_ref, out_ref):
    width = x_ref.shape[2]
    rows_out, cols_out = out_ref.shape
    for j in range(x_ref.shape[0]):
        part, at = x_ref[j].astype(f32), j * width
        if at < qkv_ref.shape[1]:
            qkv_ref[:, at : at + width] = part
        else:
            at -= qkv_ref.shape[1]
            for k in range(2):
                cols = slice(k * (cols_out // 2) + at, k * (cols_out // 2) + at + width)
                out_ref[:, cols] = part[k * rows_out : (k + 1) * rows_out]


VMEM = pl.BlockSpec(memory_space=pltpu.VMEM)
SMEM = pl.BlockSpec(memory_space=pltpu.SMEM)
ANY = pl.BlockSpec(memory_space=pl.ANY)


def kernel(body, outs, name, flops, in_specs=None, scratch=(), room=None):
    many = isinstance(outs, (list, tuple))
    every = list(outs) if many else [outs]
    size = sum(math.prod(o.shape) * o.dtype.itemsize for o in every)

    def call(*args):
        return pl.pallas_call(
            body,
            out_shape=every if many else outs,
            in_specs=in_specs or [VMEM] * len(args),
            out_specs=[VMEM] * len(every) if many else VMEM,
            scratch_shapes=list(scratch),
            cost_estimate=pl.CostEstimate(
                flops=flops,
                bytes_accessed=size + sum(math.prod(a.shape) * a.dtype.itemsize for a in args),
                transcendentals=0,
            ),
            compiler_params=pltpu.CompilerParams(vmem_limit_bytes=room),
            name=name,
        )(*args)

    return call


def shape(dims, dtype=bf16):
    return jax.ShapeDtypeStruct(tuple(dims), dtype)


def to_all(x, axis):
    return lax.all_to_all(x, axis, 0, 0, tiled=True)


def turned(x, axis, k):
    n = lax.axis_size(axis)
    return lax.ppermute(x, axis, [(i, (i + k) % n) for i in range(n)])


def depth_call(weight, place, attended, embedded, codes, gain, w_in, table, weights):
    frames, positions = codes.shape
    width, entries, rows = w_in.shape[1], table.shape[0], frames * positions
    dh = (weights[0].shape[2] - width // 2) // 3
    _, share, columns = weights[0].shape
    owners = len(weights)
    cut = shape((owners, share, columns))
    pairs = len(pairs_of(positions)) * frames
    return kernel(
        functools.partial(depth_body, weight=weight, head=DEPTH_HEAD),
        (cut, cut),
        "depth",
        11 * 10**9,
        room=40 << 20,
        in_specs=[SMEM] + [VMEM] * 4 + [ANY] * 10,
        scratch=[
            pltpu.VMEM(w_in.shape, bf16),
            pltpu.VMEM(table.shape, bf16),
            pltpu.VMEM((width, columns), bf16),
            pltpu.VMEM((dh, width), bf16),
            pltpu.VMEM((rows, width), f32),
            pltpu.VMEM((rows, width), bf16),
            pltpu.VMEM((width, rows), bf16),
            pltpu.VMEM((rows, 3 * dh), bf16),
            pltpu.VMEM((2 * pairs, dh), bf16),
            pltpu.VMEM((pairs, dh), f32),
            pltpu.VMEM((pairs, dh), f32),
            pltpu.VMEM((rows, dh), bf16),
            pltpu.VMEM((dh, rows), bf16),
            pltpu.VMEM((rows, 128), f32),
            pltpu.VMEM((rows, entries), f32),
            pltpu.VMEM((rows, entries), bf16),
            pltpu.VMEM((rows, width), bf16),
            pltpu.VMEM((rows, 3 * dh), bf16),
            pltpu.VMEM((owners, 2, share, 256), bf16),
            pltpu.SemaphoreType.DMA((2 * owners,)),
            pltpu.SemaphoreType.DMA((width // 256,)),
            pltpu.SemaphoreType.DMA,
        ],
    )(place, attended, embedded, codes, gain.reshape(1, width), w_in, table, *weights)


def local(query, keys, values, codes, w_in, table, gain, w_qkv, w_out):
    parts = lax.axis_size(CTX)
    frames, positions = codes.shape[1:]
    width, dh = w_in.shape[1], w_out.shape[0] * lax.axis_size(DP)
    entries = table.shape[0]
    place = jnp.stack([lax.axis_index(name) for name in DP])

    packed = kernel(pack_body, shape((parts, 3, frames, HEAD_DIM)), "pack", 1 << 20)(
        query, keys, values
    )
    w_qkv, w_out, packed = lax.optimization_barrier((w_qkv, w_out, packed))
    both = jnp.concatenate(
        [w_qkv, jnp.concatenate([w_out[:, : width // 2], w_out[:, width // 2 :]], axis=0)], axis=1
    )
    pair = jnp.stack([both, turned(both, "dp_0", 1)])
    near = [pair] + [turned(pair, "dp_1", k) for k in range(1, lax.axis_size("dp_1"))]

    moved = to_all(packed, CTX)
    embedded = kernel(
        embed_body,
        shape((positions - 1, frames, width)),
        "embed",
        2 * (positions - 1) * frames * entries * width,
        room=10 << 20,
        scratch=[pltpu.VMEM(((positions - 1) * frames, entries), bf16)],
    )(codes[0], table)

    heads = kernel(
        functools.partial(attend_body, step=2),
        shape((parts, frames, HEAD_DIM)),
        "attend",
        4 * (parts * frames) ** 2 * HEAD_DIM,
        room=24 << 20,
    )(moved)
    attended = to_all(heads, CTX)
    near, heads = lax.optimization_barrier((near, heads))
    weights = near + [turned(w, "dp_2", 1) for w in near]

    keep, send = depth_call(
        1.0 / lax.axis_size(DP), place, attended, embedded, codes[0], gain, w_in, table, weights
    )
    swapped = turned(send, "dp_2", 1)
    owners, rows, columns = keep.shape
    planes, lane = lax.axis_size("ctx_0"), columns // parts
    halves = shape((owners, planes, rows, columns // planes))
    chip_sum = kernel(add_cut_body, halves, "chip_sum", 1 << 22, room=16 << 20)(keep, swapped)
    chip_sum = chip_sum.reshape(owners * planes, rows, columns // planes)
    plane_sum = kernel(
        fold_cut_body, shape((parts // planes, rows, lane)), "plane_sum", 1 << 22, room=8 << 20
    )(to_all(chip_sum, PLANE))
    whole_sum = kernel(fold_copy_body, shape((parts, rows, lane)), "whole_sum", 1 << 20, room=4 << 20)(
        to_all(plane_sum, "ctx_1")
    )
    return kernel(
        lay_out_body, (shape(w_qkv.shape, f32), shape(w_out.shape, f32)), "lay_out", 1 << 20, room=4 << 20
    )(to_all(whole_sum, CTX))


def solution(mesh):
    torus = Mesh(mesh.devices.reshape(2, 4, 2, 2, 8), DP + CTX)
    frames = P(DP, CTX, None)
    in_specs = (frames, frames, frames, frames, P(), P(), P(), P(DP, None), P(DP, None))
    out_specs = (P(DP, None), P(DP, None))
    return jax.shard_map(local, mesh=torus, in_specs=in_specs, out_specs=out_specs, check_vma=False)
```

profile of v0, /device:TPU:32, one launch (start us, length us, event | category | flops | bytes accessed | tf_op | source)
XLA Modules:
  0.0 176.3 jit_solution(10500685792894272599)
XLA Ops:
  0.6 2.8 %pack.1 = bf16[16,3,128,128]{3,2,1,0:T(8,128)(2,1)} custom-call(bf16[1,128,2048]{2,1,0:T(8,128)(2,1)} %query_ref.1, bf16[1,128,2048]{2,1,0:T(8,128)(2,1)} %keys_ref.1, bf16[1,128,2048]{2,1,0:T(8,128)(2,1)} %values_ref.1), custom_call_target="tpu_custom_call" | custom-call | flops 1048576 | bytes 3145728 | tf_op jit(solution)/shard_map/pack/pallas_call | solution.py:328
  3.4 11.2 %all-to-all-start = ((bf16[16,3,128,128]{3,2,1,0:T(8,128)(2,1)}), bf16[16,3,128,128]{3,2,1,0:T(8,128)(2,1)S(1)}, u32[]{:S(2)}, u32[]{:S(2)}) async-start(bf16[16,3,128,128]{3,2,1,0:T(8,128)(2,1)} %pack.1), calls=%async_computation | async-start | bytes 3145728 | tf_op jit(solution)/shard_map/all_to_all | solution.py:351
  14.7 0.7 collective-permute-start
  15.4 11.6 %collective-permute-done = bf16[64,2048]{1,0:T(8,128)(2,1)S(1)} collective-permute-done((bf16[64,2048]{1,0:T(8,128)(2,1)S(1)}, bf16[64,2048]{1,0:T(8,128)(2,1)S(1)}, u32[]{:S(2)}, u32[]{:S(2)}) %collective-permute-start) | collective-permute-done | bytes 262176 | tf_op jit(solution)/shard_map/ppermute | solution.py:356
  27.0 3.1 %collective-permute-start.3 = (bf16[2,64,2048]{2,1,0:T(8,128)(2,1)S(1)}, bf16[2,64,2048]{2,1,0:T(8,128)(2,1)S(1)}, u32[]{:S(2)}, u32[]{:S(2)}) collective-permute-start(bf16[2,64,2048]{2,1,0:T(8,128)(2,1)S(1)} %pad_maximum_fusion.w0_hbm), channel_id=1, source_target_pairs={{0,96},{32,0},{64,32},{96,64},{1,97},{33,1},{65,33},{97,65},{2,98}... | collective-permute-start | bytes 1572872 | tf_op jit(solution)/shard_map/ppermute | solution.py:356
  30.1 0.6 collective-permute-start.2
  30.7 1.0 collective-permute-start.1
  31.7 22.0 %all-to-all-done.x_ref = bf16[16,3,128,128]{3,2,1,0:T(8,128)(2,1)S(1)} async-done(((bf16[16,3,128,128]{3,2,1,0:T(8,128)(2,1)}), bf16[16,3,128,128]{3,2,1,0:T(8,128)(2,1)S(1)}, u32[]{:S(2)}, u32[]{:S(2)}) %all-to-all-start) | async-done | bytes 1572896 | tf_op jit(solution)/shard_map/all_to_all | solution.py:351
  53.7 5.6 %attend.1 = bf16[16,128,128]{2,1,0:T(8,128)(2,1)} custom-call(bf16[16,3,128,128]{3,2,1,0:T(8,128)(2,1)S(1)} %all-to-all-done.x_ref), custom_call_target="tpu_custom_call" | custom-call | flops 2147483648 | bytes 2097152 | tf_op jit(solution)/shard_map/attend/pallas_call | solution.py:328
  59.4 5.4 %all-to-all-start.1 = ((bf16[16,128,128]{2,1,0:T(8,128)(2,1)}), bf16[16,128,128]{2,1,0:T(8,128)(2,1)S(1)}, u32[]{:S(2)}, u32[]{:S(2)}) async-start(bf16[16,128,128]{2,1,0:T(8,128)(2,1)} %attend.1), calls=%async_computation.1 | async-start | bytes 1048576 | tf_op jit(solution)/shard_map/all_to_all | solution.py:351
  64.9 0.5 collective-permute-start.5
  66.1 2.2 %copy-done = bf16[2048,1024]{1,0:T(8,128)(2,1)S(1)} copy-done((bf16[2048,1024]{1,0:T(8,128)(2,1)S(1)}, bf16[2048,1024]{1,0:T(8,128)(2,1)}, u32[]{:S(2)}) %copy-start) | copy-done | bytes 4194328
  68.3 2.7 %embed.1.emb_ref = bf16[3,128,1024]{2,1,0:T(8,128)(2,1)S(1)} custom-call(s32[128,4]{1,0:T(8,128)S(1)} %bitcast.10, bf16[2048,1024]{1,0:T(8,128)(2,1)S(1)} %copy-done), custom_call_target="tpu_custom_call" | custom-call | flops 1610612736 | bytes 4982784 | tf_op jit(solution)/shard_map/embed/pallas_call | solution.py:328
  71.1 0.9 copy-done.3
  72.0 9.2 %all-to-all-done.1.att_ref = bf16[16,128,128]{2,1,0:T(8,128)(2,1)S(1)} async-done(((bf16[16,128,128]{2,1,0:T(8,128)(2,1)}), bf16[16,128,128]{2,1,0:T(8,128)(2,1)S(1)}, u32[]{:S(2)}, u32[]{:S(2)}) %all-to-all-start.1) | async-done | bytes 524320 | tf_op jit(solution)/shard_map/all_to_all | solution.py:351
  81.2 2.2 %copy-done.1 = bf16[2048,1024]{1,0:T(8,128)(2,1)S(1)} copy-done((bf16[2048,1024]{1,0:T(8,128)(2,1)S(1)}, bf16[2048,1024]{1,0:T(8,128)(2,1)}, u32[]{:S(2)}) %copy-start.1) | copy-done | bytes 4194328
  83.3 1.1 copy-done.4
  84.5 25.8 %depth.1 = (bf16[8,64,2048]{2,1,0:T(8,128)(2,1)S(1)}, bf16[8,64,2048]{2,1,0:T(8,128)(2,1)S(1)}) custom-call(s32[3]{0:T(128)S(1)} %pad_add_fusion.place_ref, bf16[16,128,128]{2,1,0:T(8,128)(2,1)S(1)} %all-to-all-done.1.att_ref, bf16[3,128,1024]{2,1,0:T(8,128)(2,1)S(1)} %copy-done.4, s32[128,4]{1,0:T(8,128)S(1)} %bitcast.11, f32[1,1024]{1,0:T(1,128)S(1)} %bitcast.12, ...), custom_call_target="tpu_custom_call" | custom-call | flops 11000000512 | bytes 18094092 | tf_op jit(solution)/shard_map/depth/pallas_call | solution.py:328
  110.4 4.1 %collective-permute-done.8.b_ref = bf16[8,64,2048]{2,1,0:T(8,128)(2,1)S(1)} collective-permute-done((bf16[8,64,2048]{2,1,0:T(8,128)(2,1)S(1)}, bf16[8,64,2048]{2,1,0:T(8,128)(2,1)S(1)}, u32[]{:S(2)}, u32[]{:S(2)}) %collective-permute-start.8) | collective-permute-done | bytes 2097184 | tf_op jit(solution)/shard_map/ppermute | solution.py:356
  114.5 0.5 chip_sum.1
  115.0 33.9 %all_to_all.25.x_ref = bf16[16,64,1024]{2,1,0:T(8,128)(2,1)S(1)} all-to-all(bf16[16,64,1024]{2,1,0:T(8,128)(2,1)S(1)} %bitcast.9), channel_id=1, replica_groups=mesh['dp_0'=2,'dp_1'=4,'dp_2'=2,'ctx_0'=2,'ctx_1'=8] {'dp_0','dp_1','ctx..., dimensions={0} | all-to-all | bytes 4194304 | tf_op jit(solution)/shard_map/all_to_all | solution.py:351
  149.3 11.5 %all_to_all.26.x_ref = bf16[8,64,128]{2,1,0:T(8,128)(2,1)S(1)} all-to-all(bf16[8,64,128]{2,1,0:T(8,128)(2,1)S(1)} %plane_sum.1), channel_id=1, replica_groups=mesh['dp_0'=2,'dp_1'=4,'dp_2'=2,'ctx_0'=2,'ctx_1'=8] {'ctx_1'}, dimensions={0} | all-to-all | bytes 262144 | tf_op jit(solution)/shard_map/all_to_all | solution.py:351
  160.8 14.7 %all_to_all.27.x_ref = bf16[16,64,128]{2,1,0:T(8,128)(2,1)S(1)} all-to-all(bf16[16,64,128]{2,1,0:T(8,128)(2,1)S(1)} %whole_sum.1), channel_id=1, replica_groups=mesh['dp_0'=2,'dp_1'=4,'dp_2'=2,'ctx_0'=2,'ctx_1'=8] {'ctx_0','ctx_1'}, dimensions={0} | all-to-all | bytes 524288 | tf_op jit(solution)/shard_map/all_to_all | solution.py:351
  175.5 0.8 lay_out.1
  (30 shorter events, 1.4 us)
Async XLA Ops:
  3.4 11.2 %copy-start.6 = (bf16[32,1024]{1,0:T(8,128)(2,1)S(1)}, bf16[32,1024]{1,0:T(8,128)(2,1)}, u32[]{:S(2)}) copy-start(bf16[32,1024]{1,0:T(8,128)(2,1)} %param.17) | copy-start | bytes 196612
  3.4 11.2 %copy-start.5 = (bf16[64,1536]{1,0:T(8,128)(2,1)S(1)}, bf16[64,1536]{1,0:T(8,128)(2,1)}, u32[]{:S(2)}) copy-start(bf16[64,1536]{1,0:T(8,128)(2,1)} %param.16) | copy-start | bytes 589828
  3.4 50.3 %all-to-all-start = ((bf16[16,3,128,128]{3,2,1,0:T(8,128)(2,1)}), bf16[16,3,128,128]{3,2,1,0:T(8,128)(2,1)S(1)}, u32[]{:S(2)}, u32[]{:S(2)}) async-start(bf16[16,3,128,128]{3,2,1,0:T(8,128)(2,1)} %pack.1), calls=%async_computation | async-start | bytes 3145728 | tf_op jit(solution)/shard_map/all_to_all | solution.py:351
  14.7 12.3 %collective-permute-start = (bf16[64,2048]{1,0:T(8,128)(2,1)S(1)}, bf16[64,2048]{1,0:T(8,128)(2,1)S(1)}, u32[]{:S(2)}, u32[]{:S(2)}) collective-permute-start(bf16[64,2048]{1,0:T(8,128)(2,1)S(1)} %get-tuple-element.21), channel_id=1, source_target_pairs={{0,128},{128,0},{1,129},{129,1},{2,130},{130,2},{3,131},{131,3},{4... | collective-permute-start | bytes 786440 | tf_op jit(solution)/shard_map/ppermute | solution.py:356
  27.0 38.9 %copy-start.7 = (s32[1,128,4]{1,2,0:T(4,128)S(1)}, s32[1,128,4]{1,2,0:T(4,128)}, u32[]{:S(2)}) copy-start(s32[1,128,4]{1,2,0:T(4,128)} %param.12) | copy-start | bytes 6148
  27.0 37.8 %collective-permute-start.3 = (bf16[2,64,2048]{2,1,0:T(8,128)(2,1)S(1)}, bf16[2,64,2048]{2,1,0:T(8,128)(2,1)S(1)}, u32[]{:S(2)}, u32[]{:S(2)}) collective-permute-start(bf16[2,64,2048]{2,1,0:T(8,128)(2,1)S(1)} %pad_maximum_fusion.w0_hbm), channel_id=1, source_target_pairs={{0,96},{32,0},{64,32},{96,64},{1,97},{33,1},{65,33},{97,65},{2,98}... | collective-permute-start | bytes 1572872 | tf_op jit(solution)/shard_map/ppermute | solution.py:356
  30.1 34.7 %collective-permute-start.2 = (bf16[2,64,2048]{2,1,0:T(8,128)(2,1)S(1)}, bf16[2,64,2048]{2,1,0:T(8,128)(2,1)S(1)}, u32[]{:S(2)}, u32[]{:S(2)}) collective-permute-start(bf16[2,64,2048]{2,1,0:T(8,128)(2,1)S(1)} %pad_maximum_fusion.w0_hbm), channel_id=1, source_target_pairs={{0,64},{32,96},{64,0},{96,32},{1,65},{33,97},{65,1},{97,33},{2,66}... | collective-permute-start | bytes 1572872 | tf_op jit(solution)/shard_map/ppermute | solution.py:356
  30.7 34.1 %collective-permute-start.1 = (bf16[2,64,2048]{2,1,0:T(8,128)(2,1)S(1)}, bf16[2,64,2048]{2,1,0:T(8,128)(2,1)}, u32[]{:S(2)}, u32[]{:S(2)}) collective-permute-start(bf16[2,64,2048]{2,1,0:T(8,128)(2,1)S(1)} %pad_maximum_fusion.w0_hbm), channel_id=1, source_target_pairs={{0,32},{32,64},{64,96},{96,0},{1,33},{33,65},{65,97},{97,1},{2,34}... | collective-permute-start | bytes 1572872 | tf_op jit(solution)/shard_map/ppermute | solution.py:356
  59.4 21.8 %all-to-all-start.1 = ((bf16[16,128,128]{2,1,0:T(8,128)(2,1)}), bf16[16,128,128]{2,1,0:T(8,128)(2,1)S(1)}, u32[]{:S(2)}, u32[]{:S(2)}) async-start(bf16[16,128,128]{2,1,0:T(8,128)(2,1)} %attend.1), calls=%async_computation.1 | async-start | bytes 1048576 | tf_op jit(solution)/shard_map/all_to_all | solution.py:351
  64.8 7.1 %collective-permute-start.4 = (bf16[2,64,2048]{2,1,0:T(8,128)(2,1)S(1)}, bf16[2,64,2048]{2,1,0:T(8,128)(2,1)S(1)}, u32[]{:S(2)}, u32[]{:S(2)}) collective-permute-start(bf16[2,64,2048]{2,1,0:T(8,128)(2,1)S(1)} %pad_maximum_fusion.w0_hbm), channel_id=1, source_target_pairs={{0,16},{16,0},{1,17},{17,1},{2,18},{18,2},{3,19},{19,3},{4,20},{20... | collective-permute-start | bytes 1572872 | tf_op jit(solution)/shard_map/ppermute | solution.py:356
  64.9 7.0 %collective-permute-start.5 = (bf16[2,64,2048]{2,1,0:T(8,128)(2,1)}, bf16[2,64,2048]{2,1,0:T(8,128)(2,1)}, u32[]{:S(2)}, u32[]{:S(2)}) collective-permute-start(bf16[2,64,2048]{2,1,0:T(8,128)(2,1)} %collective-permute-done.1.w1_hbm), channel_id=1, source_target_pairs={{0,16},{16,0},{1,17},{17,1},{2,18},{18,2},{3,19},{19,3},{4,20},{20... | collective-permute-start | bytes 1572872 | tf_op jit(solution)/shard_map/ppermute | solution.py:356
  65.4 6.5 %collective-permute-start.6 = (bf16[2,64,2048]{2,1,0:T(8,128)(2,1)S(1)}, bf16[2,64,2048]{2,1,0:T(8,128)(2,1)}, u32[]{:S(2)}, u32[]{:S(2)}) collective-permute-start(bf16[2,64,2048]{2,1,0:T(8,128)(2,1)S(1)} %collective-permute-done.2.w2_hbm), channel_id=1, source_target_pairs={{0,16},{16,0},{1,17},{17,1},{2,18},{18,2},{3,19},{19,3},{4,20},{20... | collective-permute-start | bytes 1572872 | tf_op jit(solution)/shard_map/ppermute | solution.py:356
  65.5 6.4 %collective-permute-start.7 = (bf16[2,64,2048]{2,1,0:T(8,128)(2,1)S(1)}, bf16[2,64,2048]{2,1,0:T(8,128)(2,1)}, u32[]{:S(2)}, u32[]{:S(2)}) collective-permute-start(bf16[2,64,2048]{2,1,0:T(8,128)(2,1)S(1)} %collective-permute-done.3.w3_hbm), channel_id=1, source_target_pairs={{0,16},{16,0},{1,17},{17,1},{2,18},{18,2},{3,19},{19,3},{4,20},{20... | collective-permute-start | bytes 1572872 | tf_op jit(solution)/shard_map/ppermute | solution.py:356
  66.1 2.2 %copy-start = (bf16[2048,1024]{1,0:T(8,128)(2,1)S(1)}, bf16[2048,1024]{1,0:T(8,128)(2,1)}, u32[]{:S(2)}) copy-start(bf16[2048,1024]{1,0:T(8,128)(2,1)} %table_hbm.1) | copy-start | bytes 12582916
  68.3 12.8 %copy-start.2 = (f32[1024]{0:T(1024)S(1)}, f32[1024]{0:T(1024)}, u32[]{:S(2)}) copy-start(f32[1024]{0:T(1024)} %param.15) | copy-start | bytes 12292
  71.1 0.9 copy-start.3
  81.2 2.2 %copy-start.1 = (bf16[2048,1024]{1,0:T(8,128)(2,1)S(1)}, bf16[2048,1024]{1,0:T(8,128)(2,1)}, u32[]{:S(2)}) copy-start(bf16[2048,1024]{1,0:T(8,128)(2,1)} %w_in_hbm.1) | copy-start | bytes 12582916
  83.3 1.1 copy-start.4
  110.2 4.2 %collective-permute-start.8 = (bf16[8,64,2048]{2,1,0:T(8,128)(2,1)S(1)}, bf16[8,64,2048]{2,1,0:T(8,128)(2,1)S(1)}, u32[]{:S(2)}, u32[]{:S(2)}) collective-permute-start(bf16[8,64,2048]{2,1,0:T(8,128)(2,1)S(1)} %get-tuple-element.19), channel_id=1, source_target_pairs={{0,16},{16,0},{1,17},{17,1},{2,18},{18,2},{3,19},{19,3},{4,20},{20... | collective-permute-start | bytes 6291464 | tf_op jit(solution)/shard_map/ppermute | solution.py:356
where the time goes:
time: 177 us; the launch traced here: 176 us
  blocking collectives  60.1 us (34%)
  waiting for transfers between devices  46.9 us (26%)
  Pallas kernels  38.6 us (22%)
  starting transfers between devices  23.2 us (13%)
  local copies, waits for them, and re-layouts  6.52 us (4%)
    all_to_all x3, blocking collectives, to_all(): return lax.all_to_all(x, axis, 0, 0, tiled=True)  60.1 us
    pallas_call x8, Pallas kernels, call(): pl.pallas_call(body, out_shape=every if many else outs, in_specs=in_specs...  38.6 us
    all_to_all x2, waiting for transfers between devices, to_all(): return lax.all_to_all(x, axis, 0, 0, tiled=True)  31.2 us
    all_to_all x2, starting transfers between devices, to_all(): return lax.all_to_all(x, axis, 0, 0, tiled=True)  16.6 us
    ppermute x9, waiting for transfers between devices, turned(): return lax.ppermute(x, axis, [(i, (i + k) % n) for i in range(n)])  15.7 us
    ppermute x9, starting transfers between devices, turned(): return lax.ppermute(x, axis, [(i, (i + k) % n) for i in range(n)])  6.56 us
    unnamed x17, local copies, waits for them, and re-layouts  6.52 us
  transfers between devices with their start and end apart: 11, of which 4 were waited for; matrix products, arithmetic and copies ran while one was open for 0% of the time, Pallas kernels for 5%

commit v1 on v0

--- a/solution.py
+++ b/solution.py
@@ -88,8 +88,8 @@
 
 
 def depth_body(
-    place_ref, att_ref, emb_ref, codes_ref, gain_ref, w_in_hbm, table_hbm, w0_hbm, w1_hbm, w2_hbm, w3_hbm,
-    t0_hbm, t1_hbm, t2_hbm, t3_hbm, keep_ref, send_ref,
+    place_ref, att_ref, emb_ref, codes_ref, gain_ref, w_in_hbm, table_hbm,
+    near_hbm, far_hbm, near_twin_hbm, far_twin_hbm, keep_ref, send_ref,
     w_in_ref, table_ref, w_ref, w_out_ref, x_ref, n_ref, n_t_ref, qkv_ref, term_ref, s_ref, p_ref, mix_ref, mix_t_ref, inv_ref,
     logit_ref, g_ref, dr_ref, dqkv_ref, stage_ref, sems, in_sems, table_sem,
     *, weight, head,
@@ -116,16 +116,16 @@
     for j in range(width // tile):
         load_in(j).start()
     loads = []
-    mine, twins = (w0_hbm, w1_hbm, w2_hbm, w3_hbm), (t0_hbm, t1_hbm, t2_hbm, t3_hbm)
-    for twin, refs in enumerate((mine, twins)):
-        for back, ref in enumerate(refs):
-            for plane in range(2):
-                at = (place_ref[0] + plane) % 2
-                at = at * len(refs) + (place_ref[1] + len(refs) - back) % len(refs)
-                at = at * 2 + (side + twin) % 2
-                rows = pl.ds(pl.multiple_of(at * rows_qkv, rows_qkv), rows_qkv)
-                loads.append(pltpu.make_async_copy(ref.at[plane], w_ref.at[rows], sems.at[len(loads)]))
-                loads[-1].start()
+    ring = near_hbm.shape[0]
+    quarters = ((0, 0, near_hbm), (0, 1, far_hbm), (1, 0, near_twin_hbm), (1, 1, far_twin_hbm))
+    for twin, plane, ref in quarters:
+        for back in range(ring):
+            at = (place_ref[0] + plane) % 2
+            at = at * ring + (place_ref[1] + ring - back) % ring
+            at = at * 2 + (side + twin) % 2
+            rows = pl.ds(pl.multiple_of(at * rows_qkv, rows_qkv), rows_qkv)
+            loads.append(pltpu.make_async_copy(ref.at[back], w_ref.at[rows], sems.at[len(loads)]))
+            loads[-1].start()
     load_table.start()
     att = jnp.concatenate([att_ref[h] for h in range(att_ref.shape[0])], axis=1)
 
@@ -271,11 +271,22 @@
         send_ref[:, :, cols] = stage_ref[:, 1 - side]
 
 
-def pack_body(query_ref, keys_ref, values_ref, o_ref):
-    for d in range(o_ref.shape[0]):
-        cols = slice(d * o_ref.shape[3], (d + 1) * o_ref.shape[3])
-        for k, ref in enumerate((query_ref, keys_ref, values_ref)):
-            o_ref[d, k] = ref[0, :, cols]
+def pack_body(query_hbm, keys_hbm, values_hbm, o_hbm, in_ref, out_ref, in_sems, out_sems):
+    sources = (query_hbm, keys_hbm, values_hbm)
+    loads = [pltpu.make_async_copy(s.at[0], in_ref.at[k], in_sems.at[k]) for k, s in enumerate(sources)]
+    stores = [
+        pltpu.make_async_copy(out_ref.at[:, k], o_hbm.at[:, k], out_sems.at[k]) for k in range(len(sources))
+    ]
+    for load in loads:
+        load.start()
+    width = out_ref.shape[3]
+    for k in range(len(sources)):
+        loads[k].wait()
+        for d in range(out_ref.shape[0]):
+            out_ref[d, k] = in_ref[k, :, d * width : (d + 1) * width]
+        stores[k].start()
+    for store in stores:
+        store.wait()
 
 
 def add_cut_body(a_ref, b_ref, o_ref):
@@ -316,10 +327,10 @@
 
 VMEM = pl.BlockSpec(memory_space=pltpu.VMEM)
 SMEM = pl.BlockSpec(memory_space=pltpu.SMEM)
-ANY = pl.BlockSpec(memory_space=pl.ANY)
-
-
-def kernel(body, outs, name, flops, in_specs=None, scratch=(), room=None):
+HBM = pl.BlockSpec(memory_space=pltpu.HBM)
+
+
+def kernel(body, outs, name, flops, in_specs=None, out_specs=None, scratch=(), room=None):
     many = isinstance(outs, (list, tuple))
     every = list(outs) if many else [outs]
     size = sum(math.prod(o.shape) * o.dtype.itemsize for o in every)
@@ -329,7 +340,7 @@
             body,
             out_shape=every if many else outs,
             in_specs=in_specs or [VMEM] * len(args),
-            out_specs=[VMEM] * len(every) if many else VMEM,
+            out_specs=out_specs or ([VMEM] * len(every) if many else VMEM),
             scratch_shapes=list(scratch),
             cost_estimate=pl.CostEstimate(
                 flops=flops,
@@ -360,8 +371,8 @@
     frames, positions = codes.shape
     width, entries, rows = w_in.shape[1], table.shape[0], frames * positions
     dh = (weights[0].shape[2] - width // 2) // 3
-    _, share, columns = weights[0].shape
-    owners = len(weights)
+    ring, share, columns = weights[0].shape
+    owners = 2 * ring
     cut = shape((owners, share, columns))
     pairs = len(pairs_of(positions)) * frames
     return kernel(
@@ -369,8 +380,8 @@
         (cut, cut),
         "depth",
         11 * 10**9,
-        room=40 << 20,
-        in_specs=[SMEM] + [VMEM] * 4 + [ANY] * 10,
+        room=44 << 20,
+        in_specs=[SMEM] + [VMEM] * 4 + [HBM] * 6,
         scratch=[
             pltpu.VMEM(w_in.shape, bf16),
             pltpu.VMEM(table.shape, bf16),
@@ -405,15 +416,29 @@
     entries = table.shape[0]
     place = jnp.stack([lax.axis_index(name) for name in DP])
 
-    packed = kernel(pack_body, shape((parts, 3, frames, HEAD_DIM)), "pack", 1 << 20)(
-        query, keys, values
-    )
+    blocks = (parts, 3, frames, HEAD_DIM)
+    packed = kernel(
+        pack_body,
+        shape(blocks),
+        "pack",
+        1 << 20,
+        in_specs=[HBM] * 3,
+        out_specs=HBM,
+        scratch=[
+            pltpu.VMEM((3, *query.shape[1:]), bf16),
+            pltpu.VMEM(blocks, bf16),
+            pltpu.SemaphoreType.DMA((3,)),
+            pltpu.SemaphoreType.DMA((3,)),
+        ],
+    )(query, keys, values)
     w_qkv, w_out, packed = lax.optimization_barrier((w_qkv, w_out, packed))
     both = jnp.concatenate(
         [w_qkv, jnp.concatenate([w_out[:, : width // 2], w_out[:, width // 2 :]], axis=0)], axis=1
     )
-    pair = jnp.stack([both, turned(both, "dp_0", 1)])
-    near = [pair] + [turned(pair, "dp_1", k) for k in range(1, lax.axis_size("dp_1"))]
+    ring = lax.axis_size("dp_1")
+    planes = [[w] + [turned(w, "dp_1", k) for k in range(1, ring)] for w in (both, turned(both, "dp_0", 1))]
+    weights = [jnp.stack(plane) for plane in planes]
+    weights += [turned(w, "dp_2", 1) for w in weights]
 
     moved = to_all(packed, CTX)
     embedded = kernel(
@@ -433,8 +458,6 @@
         room=24 << 20,
     )(moved)
     attended = to_all(heads, CTX)
-    near, heads = lax.optimization_barrier((near, heads))
-    weights = near + [turned(w, "dp_2", 1) for w in near]
 
     keep, send = depth_call(
         1.0 / lax.axis_size(DP), place, attended, embedded, codes[0], gain, w_in, table, weights

time: 177 us -> 173 us (0.977)
  local copies, waits for them, and re-layouts: 6.52 us -> 2.33 us
  waiting for transfers between devices: 46.9 us -> 43.2 us
  starting transfers between devices: 23.2 us -> 26.7 us
    all_to_all x2, waiting for transfers between devices: 31.2 us -> 20.2 us  [to_all(): return lax.all_to_all(x, axis, 0, 0, tiled=True)]
    ppermute x9 -> x10, waiting for transfers between devices: 15.7 us -> 23 us  [turned(): return lax.ppermute(x, axis, [(i, (i + k) % n) for i in range(n)])]
    unnamed x17 -> x11, local copies, waits for them, and re-layouts: 6.52 us -> 2.32 us
    ppermute x9 -> x10, starting transfers between devices: 6.56 us -> 10.1 us  [turned(): return lax.ppermute(x, axis, [(i, (i + k) % n) for i in range(n)])]
  transfers between devices with their start and end apart: 11 -> 12, of which waited for: 4 -> 8; matrix products, arithmetic and copies ran while one was open for 0% -> 1% of each run, Pallas kernels for 5% -> 5%
where the time goes in v1:
time: 173 us; the launch traced here: 172 us
  blocking collectives  60 us (35%)
  waiting for transfers between devices  43.2 us (25%)
  Pallas kernels  37.9 us (22%)
  starting transfers between devices  26.7 us (15%)
  local copies, waits for them, and re-layouts  2.33 us (1%)
    all_to_all x3, blocking collectives, to_all(): return lax.all_to_all(x, axis, 0, 0, tiled=True)  60 us
    pallas_call x8, Pallas kernels, call(): pl.pallas_call(body, out_shape=every if many else outs, in_specs=in_specs...  37.9 us
    ppermute x10, waiting for transfers between devices, turned(): return lax.ppermute(x, axis, [(i, (i + k) % n) for i in range(n)])  23 us
    all_to_all x2, waiting for transfers between devices, to_all(): return lax.all_to_all(x, axis, 0, 0, tiled=True)  20.2 us
    all_to_all x2, starting transfers between devices, to_all(): return lax.all_to_all(x, axis, 0, 0, tiled=True)  16.6 us
    ppermute x10, starting transfers between devices, turned(): return lax.ppermute(x, axis, [(i, (i + k) % n) for i in range(n)])  10.1 us
  transfers between devices with their start and end apart: 12, of which 8 were waited for; matrix products, arithmetic and copies ran while one was open for 1% of the time, Pallas kernels for 5%

profile of v1, /device:TPU:32, one launch (start us, length us, event | category | flops | bytes accessed | tf_op | source)
XLA Modules:
  0.0 172.2 jit_solution(18249975808866238953)
XLA Ops:
  0.6 2.4 %pack.1 = bf16[16,3,128,128]{3,2,1,0:T(8,128)(2,1)} custom-call(bf16[1,128,2048]{2,1,0:T(8,128)(2,1)} %query_hbm.1, bf16[1,128,2048]{2,1,0:T(8,128)(2,1)} %keys_hbm.1, bf16[1,128,2048]{2,1,0:T(8,128)(2,1)} %values_hbm.1), custom_call_target="tpu_custom_call" | custom-call | flops 1048576 | bytes 3145728 | tf_op jit(solution)/shard_map/pack/pallas_call | solution.py:339
  3.0 11.2 %all-to-all-start = ((bf16[16,3,128,128]{3,2,1,0:T(8,128)(2,1)}), bf16[16,3,128,128]{3,2,1,0:T(8,128)(2,1)S(1)}, u32[]{:S(2)}, u32[]{:S(2)}) async-start(bf16[16,3,128,128]{3,2,1,0:T(8,128)(2,1)} %pack.1), calls=%async_computation | async-start | bytes 3145728 | tf_op jit(solution)/shard_map/all_to_all | solution.py:362
  14.3 0.7 collective-permute-start.3
  15.0 3.0 %collective-permute-start.2 = (bf16[64,2048]{1,0:T(8,128)(2,1)S(1)}, bf16[64,2048]{1,0:T(8,128)(2,1)S(1)}, u32[]{:S(2)}, u32[]{:S(2)}) collective-permute-start(bf16[64,2048]{1,0:T(8,128)(2,1)S(1)} %get-tuple-element.13), channel_id=1, source_target_pairs={{0,96},{32,0},{64,32},{96,64},{1,97},{33,1},{65,33},{97,65},{2,98}... | collective-permute-start | bytes 786440 | tf_op jit(solution)/shard_map/ppermute | solution.py:367
  18.6 1.0 collective-permute-start
  19.6 7.0 %collective-permute-done.3 = bf16[64,2048]{1,0:T(8,128)(2,1)S(1)} collective-permute-done((bf16[64,2048]{1,0:T(8,128)(2,1)S(1)}, bf16[64,2048]{1,0:T(8,128)(2,1)S(1)}, u32[]{:S(2)}, u32[]{:S(2)}) %collective-permute-start.3) | collective-permute-done | bytes 262176 | tf_op jit(solution)/shard_map/ppermute | solution.py:367
  26.5 3.0 %collective-permute-start.6 = (bf16[64,2048]{1,0:T(8,128)(2,1)S(1)}, bf16[64,2048]{1,0:T(8,128)(2,1)S(1)}, u32[]{:S(2)}, u32[]{:S(2)}) collective-permute-start(bf16[64,2048]{1,0:T(8,128)(2,1)S(1)} %collective-permute-done.3), channel_id=1, source_target_pairs={{0,96},{32,0},{64,32},{96,64},{1,97},{33,1},{65,33},{97,65},{2,98}... | collective-permute-start | bytes 786440 | tf_op jit(solution)/shard_map/ppermute | solution.py:367
  30.2 1.0 collective-permute-start.4
  31.1 2.0 %collective-permute-done = bf16[64,2048]{1,0:T(8,128)(2,1)S(1)} collective-permute-done((bf16[64,2048]{1,0:T(8,128)(2,1)S(1)}, bf16[64,2048]{1,0:T(8,128)(2,1)S(1)}, u32[]{:S(2)}, u32[]{:S(2)}) %collective-permute-start) | collective-permute-done | bytes 262176 | tf_op jit(solution)/shard_map/ppermute | solution.py:367
  33.4 6.2 %collective-permute-done.6 = bf16[64,2048]{1,0:T(8,128)(2,1)S(1)} collective-permute-done((bf16[64,2048]{1,0:T(8,128)(2,1)S(1)}, bf16[64,2048]{1,0:T(8,128)(2,1)S(1)}, u32[]{:S(2)}, u32[]{:S(2)}) %collective-permute-start.6) | collective-permute-done | bytes 262176 | tf_op jit(solution)/shard_map/ppermute | solution.py:367
  40.2 3.0 %collective-permute-done.4 = bf16[64,2048]{1,0:T(8,128)(2,1)S(1)} collective-permute-done((bf16[64,2048]{1,0:T(8,128)(2,1)S(1)}, bf16[64,2048]{1,0:T(8,128)(2,1)S(1)}, u32[]{:S(2)}, u32[]{:S(2)}) %collective-permute-start.4) | collective-permute-done | bytes 262176 | tf_op jit(solution)/shard_map/ppermute | solution.py:367
  43.3 1.1 pad_maximum_fusion.1.far_hbm
  44.4 8.9 %all-to-all-done.x_ref = bf16[16,3,128,128]{3,2,1,0:T(8,128)(2,1)S(1)} async-done(((bf16[16,3,128,128]{3,2,1,0:T(8,128)(2,1)}), bf16[16,3,128,128]{3,2,1,0:T(8,128)(2,1)S(1)}, u32[]{:S(2)}, u32[]{:S(2)}) %all-to-all-start) | async-done | bytes 1572896 | tf_op jit(solution)/shard_map/all_to_all | solution.py:362
  53.3 5.7 %attend.1 = bf16[16,128,128]{2,1,0:T(8,128)(2,1)} custom-call(bf16[16,3,128,128]{3,2,1,0:T(8,128)(2,1)S(1)} %all-to-all-done.x_ref), custom_call_target="tpu_custom_call" | custom-call | flops 2147483648 | bytes 2097152 | tf_op jit(solution)/shard_map/attend/pallas_call | solution.py:339
  59.0 5.5 %all-to-all-start.1 = ((bf16[16,128,128]{2,1,0:T(8,128)(2,1)}), bf16[16,128,128]{2,1,0:T(8,128)(2,1)S(1)}, u32[]{:S(2)}, u32[]{:S(2)}) async-start(bf16[16,128,128]{2,1,0:T(8,128)(2,1)} %attend.1), calls=%async_computation.1 | async-start | bytes 1048576 | tf_op jit(solution)/shard_map/all_to_all | solution.py:362
  64.6 2.2 %copy-done = bf16[2048,1024]{1,0:T(8,128)(2,1)S(1)} copy-done((bf16[2048,1024]{1,0:T(8,128)(2,1)S(1)}, bf16[2048,1024]{1,0:T(8,128)(2,1)}, u32[]{:S(2)}) %copy-start) | copy-done | bytes 4194328
  66.8 2.7 %embed.1.emb_ref = bf16[3,128,1024]{2,1,0:T(8,128)(2,1)S(1)} custom-call(s32[128,4]{1,0:T(8,128)S(1)} %bitcast.16, bf16[2048,1024]{1,0:T(8,128)(2,1)S(1)} %copy-done), custom_call_target="tpu_custom_call" | custom-call | flops 1610612736 | bytes 4982784 | tf_op jit(solution)/shard_map/embed/pallas_call | solution.py:339
  69.6 11.2 %all-to-all-done.1.att_ref = bf16[16,128,128]{2,1,0:T(8,128)(2,1)S(1)} async-done(((bf16[16,128,128]{2,1,0:T(8,128)(2,1)}), bf16[16,128,128]{2,1,0:T(8,128)(2,1)S(1)}, u32[]{:S(2)}, u32[]{:S(2)}) %all-to-all-start.1) | async-done | bytes 524320 | tf_op jit(solution)/shard_map/all_to_all | solution.py:362
  80.8 25.5 %depth.1 = (bf16[8,64,2048]{2,1,0:T(8,128)(2,1)S(1)}, bf16[8,64,2048]{2,1,0:T(8,128)(2,1)S(1)}) custom-call(s32[3]{0:T(128)S(1)} %pad_add_fusion.place_ref, bf16[16,128,128]{2,1,0:T(8,128)(2,1)S(1)} %all-to-all-done.1.att_ref, bf16[3,128,1024]{2,1,0:T(8,128)(2,1)S(1)} %embed.1.emb_ref, s32[128,4]{1,0:T(8,128)S(1)} %bitcast.17, f32[1,1024]{1,0:T(1,128)S(1)} %bitcast.18, ...), custom_call_target="tpu_custom_call" | custom-call | flops 11000000512 | bytes 18094092 | tf_op jit(solution)/shard_map/depth/pallas_call | solution.py:339
  106.4 4.1 %collective-permute-done.9.b_ref = bf16[8,64,2048]{2,1,0:T(8,128)(2,1)S(1)} collective-permute-done((bf16[8,64,2048]{2,1,0:T(8,128)(2,1)S(1)}, bf16[8,64,2048]{2,1,0:T(8,128)(2,1)S(1)}, u32[]{:S(2)}, u32[]{:S(2)}) %collective-permute-start.9) | collective-permute-done | bytes 2097184 | tf_op jit(solution)/shard_map/ppermute | solution.py:367
  111.0 33.7 %all_to_all.25.x_ref = bf16[16,64,1024]{2,1,0:T(8,128)(2,1)S(1)} all-to-all(bf16[16,64,1024]{2,1,0:T(8,128)(2,1)S(1)} %bitcast.15), channel_id=1, replica_groups=mesh['dp_0'=2,'dp_1'=4,'dp_2'=2,'ctx_0'=2,'ctx_1'=8] {'dp_0','dp_1','ctx..., dimensions={0} | all-to-all | bytes 4194304 | tf_op jit(solution)/shard_map/all_to_all | solution.py:362
  145.1 11.6 %all_to_all.26.x_ref = bf16[8,64,128]{2,1,0:T(8,128)(2,1)S(1)} all-to-all(bf16[8,64,128]{2,1,0:T(8,128)(2,1)S(1)} %plane_sum.1), channel_id=1, replica_groups=mesh['dp_0'=2,'dp_1'=4,'dp_2'=2,'ctx_0'=2,'ctx_1'=8] {'ctx_1'}, dimensions={0} | all-to-all | bytes 262144 | tf_op jit(solution)/shard_map/all_to_all | solution.py:362
  156.7 14.7 %all_to_all.27.x_ref = bf16[16,64,128]{2,1,0:T(8,128)(2,1)S(1)} all-to-all(bf16[16,64,128]{2,1,0:T(8,128)(2,1)S(1)} %whole_sum.1), channel_id=1, replica_groups=mesh['dp_0'=2,'dp_1'=4,'dp_2'=2,'ctx_0'=2,'ctx_1'=8] {'ctx_0','ctx_1'}, dimensions={0} | all-to-all | bytes 524288 | tf_op jit(solution)/shard_map/all_to_all | solution.py:362
  171.4 0.8 lay_out.1
  (27 shorter events, 3.4 us)
Async XLA Ops:
  3.0 11.2 %copy-start.3 = (bf16[32,1024]{1,0:T(8,128)(2,1)S(1)}, bf16[32,1024]{1,0:T(8,128)(2,1)}, u32[]{:S(2)}) copy-start(bf16[32,1024]{1,0:T(8,128)(2,1)} %param.17) | copy-start | bytes 196612
  3.0 11.2 %copy-start.2 = (bf16[64,1536]{1,0:T(8,128)(2,1)S(1)}, bf16[64,1536]{1,0:T(8,128)(2,1)}, u32[]{:S(2)}) copy-start(bf16[64,1536]{1,0:T(8,128)(2,1)} %param.16) | copy-start | bytes 589828
  3.0 50.3 %all-to-all-start = ((bf16[16,3,128,128]{3,2,1,0:T(8,128)(2,1)}), bf16[16,3,128,128]{3,2,1,0:T(8,128)(2,1)S(1)}, u32[]{:S(2)}, u32[]{:S(2)}) async-start(bf16[16,3,128,128]{3,2,1,0:T(8,128)(2,1)} %pack.1), calls=%async_computation | async-start | bytes 3145728 | tf_op jit(solution)/shard_map/all_to_all | solution.py:362
  14.3 12.2 %collective-permute-start.3 = (bf16[64,2048]{1,0:T(8,128)(2,1)S(1)}, bf16[64,2048]{1,0:T(8,128)(2,1)S(1)}, u32[]{:S(2)}, u32[]{:S(2)}) collective-permute-start(bf16[64,2048]{1,0:T(8,128)(2,1)S(1)} %get-tuple-element.13), channel_id=1, source_target_pairs={{0,128},{128,0},{1,129},{129,1},{2,130},{130,2},{3,131},{131,3},{4... | collective-permute-start | bytes 786440 | tf_op jit(solution)/shard_map/ppermute | solution.py:367
  15.0 15.2 %collective-permute-start.2 = (bf16[64,2048]{1,0:T(8,128)(2,1)S(1)}, bf16[64,2048]{1,0:T(8,128)(2,1)S(1)}, u32[]{:S(2)}, u32[]{:S(2)}) collective-permute-start(bf16[64,2048]{1,0:T(8,128)(2,1)S(1)} %get-tuple-element.13), channel_id=1, source_target_pairs={{0,96},{32,0},{64,32},{96,64},{1,97},{33,1},{65,33},{97,65},{2,98}... | collective-permute-start | bytes 786440 | tf_op jit(solution)/shard_map/ppermute | solution.py:367
  18.0 13.2 %collective-permute-start.1 = (bf16[64,2048]{1,0:T(8,128)(2,1)S(1)}, bf16[64,2048]{1,0:T(8,128)(2,1)S(1)}, u32[]{:S(2)}, u32[]{:S(2)}) collective-permute-start(bf16[64,2048]{1,0:T(8,128)(2,1)S(1)} %get-tuple-element.13), channel_id=1, source_target_pairs={{0,64},{32,96},{64,0},{96,32},{1,65},{33,97},{65,1},{97,33},{2,66}... | collective-permute-start | bytes 786440 | tf_op jit(solution)/shard_map/ppermute | solution.py:367
  18.6 14.5 %collective-permute-start = (bf16[64,2048]{1,0:T(8,128)(2,1)S(1)}, bf16[64,2048]{1,0:T(8,128)(2,1)S(1)}, u32[]{:S(2)}, u32[]{:S(2)}) collective-permute-start(bf16[64,2048]{1,0:T(8,128)(2,1)S(1)} %get-tuple-element.13), channel_id=1, source_target_pairs={{0,32},{32,64},{64,96},{96,0},{1,33},{33,65},{65,97},{97,1},{2,34}... | collective-permute-start | bytes 786440 | tf_op jit(solution)/shard_map/ppermute | solution.py:367
  26.5 13.0 %collective-permute-start.6 = (bf16[64,2048]{1,0:T(8,128)(2,1)S(1)}, bf16[64,2048]{1,0:T(8,128)(2,1)S(1)}, u32[]{:S(2)}, u32[]{:S(2)}) collective-permute-start(bf16[64,2048]{1,0:T(8,128)(2,1)S(1)} %collective-permute-done.3), channel_id=1, source_target_pairs={{0,96},{32,0},{64,32},{96,64},{1,97},{33,1},{65,33},{97,65},{2,98}... | collective-permute-start | bytes 786440 | tf_op jit(solution)/shard_map/ppermute | solution.py:367
  29.5 10.7 %collective-permute-start.5 = (bf16[64,2048]{1,0:T(8,128)(2,1)S(1)}, bf16[64,2048]{1,0:T(8,128)(2,1)S(1)}, u32[]{:S(2)}, u32[]{:S(2)}) collective-permute-start(bf16[64,2048]{1,0:T(8,128)(2,1)S(1)} %collective-permute-done.3), channel_id=1, source_target_pairs={{0,64},{32,96},{64,0},{96,32},{1,65},{33,97},{65,1},{97,33},{2,66}... | collective-permute-start | bytes 786440 | tf_op jit(solution)/shard_map/ppermute | solution.py:367
  30.2 13.1 %collective-permute-start.4 = (bf16[64,2048]{1,0:T(8,128)(2,1)S(1)}, bf16[64,2048]{1,0:T(8,128)(2,1)S(1)}, u32[]{:S(2)}, u32[]{:S(2)}) collective-permute-start(bf16[64,2048]{1,0:T(8,128)(2,1)S(1)} %collective-permute-done.3), channel_id=1, source_target_pairs={{0,32},{32,64},{64,96},{96,0},{1,33},{33,65},{65,97},{97,1},{2,34}... | collective-permute-start | bytes 786440 | tf_op jit(solution)/shard_map/ppermute | solution.py:367
  33.3 36.3 %collective-permute-start.7 = (bf16[4,64,2048]{2,1,0:T(8,128)(2,1)S(1)}, bf16[4,64,2048]{2,1,0:T(8,128)(2,1)}, u32[]{:S(2)}, u32[]{:S(2)}) collective-permute-start(bf16[4,64,2048]{2,1,0:T(8,128)(2,1)S(1)} %pad_maximum_fusion.near_hbm), channel_id=1, source_target_pairs={{0,16},{16,0},{1,17},{17,1},{2,18},{18,2},{3,19},{19,3},{4,20},{20... | collective-permute-start | bytes 3145736 | tf_op jit(solution)/shard_map/ppermute | solution.py:367
  44.4 20.1 %copy-start.4 = (s32[1,128,4]{1,2,0:T(4,128)S(1)}, s32[1,128,4]{1,2,0:T(4,128)}, u32[]{:S(2)}) copy-start(s32[1,128,4]{1,2,0:T(4,128)} %param.12) | copy-start | bytes 6148
  44.4 25.2 %collective-permute-start.8 = (bf16[4,64,2048]{2,1,0:T(8,128)(2,1)}, bf16[4,64,2048]{2,1,0:T(8,128)(2,1)}, u32[]{:S(2)}, u32[]{:S(2)}) collective-permute-start(bf16[4,64,2048]{2,1,0:T(8,128)(2,1)} %pad_maximum_fusion.1.far_hbm), channel_id=1, source_target_pairs={{0,16},{16,0},{1,17},{17,1},{2,18},{18,2},{3,19},{19,3},{4,20},{20... | collective-permute-start | bytes 3145736 | tf_op jit(solution)/shard_map/ppermute | solution.py:367
  59.0 21.8 %all-to-all-start.1 = ((bf16[16,128,128]{2,1,0:T(8,128)(2,1)}), bf16[16,128,128]{2,1,0:T(8,128)(2,1)S(1)}, u32[]{:S(2)}, u32[]{:S(2)}) async-start(bf16[16,128,128]{2,1,0:T(8,128)(2,1)} %attend.1), calls=%async_computation.1 | async-start | bytes 1048576 | tf_op jit(solution)/shard_map/all_to_all | solution.py:362
  64.6 2.2 %copy-start = (bf16[2048,1024]{1,0:T(8,128)(2,1)S(1)}, bf16[2048,1024]{1,0:T(8,128)(2,1)}, u32[]{:S(2)}) copy-start(bf16[2048,1024]{1,0:T(8,128)(2,1)} %table_hbm.1) | copy-start | bytes 12582916
  66.8 14.0 %copy-start.1 = (f32[1024]{0:T(1024)S(1)}, f32[1024]{0:T(1024)}, u32[]{:S(2)}) copy-start(f32[1024]{0:T(1024)} %param.15) | copy-start | bytes 12292
  106.3 4.2 %collective-permute-start.9 = (bf16[8,64,2048]{2,1,0:T(8,128)(2,1)S(1)}, bf16[8,64,2048]{2,1,0:T(8,128)(2,1)S(1)}, u32[]{:S(2)}, u32[]{:S(2)}) collective-permute-start(bf16[8,64,2048]{2,1,0:T(8,128)(2,1)S(1)} %get-tuple-element.11), channel_id=1, source_target_pairs={{0,16},{16,0},{1,17},{17,1},{2,18},{18,2},{3,19},{19,3},{4,20},{20... | collective-permute-start | bytes 6291464 | tf_op jit(solution)/shard_map/ppermute | solution.py:367

commit v2 on v1

--- a/solution.py
+++ b/solution.py
@@ -36,12 +36,12 @@
         q = x_ref[i:seen, 0].reshape(step * rows, dim)
         k = x_ref[0:seen, 1].reshape(seen * rows, dim)
         v = x_ref[0:seen, 2].reshape(seen * rows, dim)
-        s = dot_nt(q, k) * (1.0 / math.sqrt(dim))
+        s = dot_nt(q, k)
         shape = (step * rows, step * rows)
         ok = lax.broadcasted_iota(jnp.int32, shape, 1) <= lax.broadcasted_iota(jnp.int32, shape, 0)
         last = jnp.where(ok, s[:, i * rows :], NEG)
         s = last if i == 0 else jnp.concatenate([s[:, : i * rows], last], axis=1)
-        p = jnp.exp(s - jnp.max(s, axis=1, keepdims=True))
+        p = jnp.exp2((s - jnp.max(s, axis=1, keepdims=True)) * (math.log2(math.e) / math.sqrt(dim)))
         total = jnp.sum(p, axis=1, keepdims=True)
         out = dot(p.astype(bf16), v) / total
         o_ref[i:seen] = out.astype(bf16).reshape(step, rows, dim)
@@ -64,17 +64,22 @@
         o_ref[:, :, cols] = rows.astype(bf16).reshape(count, frames, tile)
 
 
-def put_split(ref, k, frames, count, term):
+def put_split(ref, rows, term, width):
     high = term.astype(bf16)
-    ref[k * frames : (k + 1) * frames] = high
-    ref[(count + k) * frames : (count + k + 1) * frames] = (term - high.astype(f32)).astype(bf16)
-
-
-def head_sums(ref, rows, heads_block, store):
-    width = heads_block.shape[0]
-    for j in range(ref.shape[1] // width):
+    low = (term - high.astype(f32)).astype(bf16)
+    for j in range(term.shape[1] // width):
         cols = slice(j * width, (j + 1) * width)
-        store(cols, dot(ref[:rows, cols], heads_block) + dot(ref[rows:, cols], heads_block))
+        ref[rows, 2 * j * width : (2 * j + 1) * width] = high[:, cols]
+        ref[rows, (2 * j + 1) * width : (2 * j + 2) * width] = low[:, cols]
+
+
+def head_sums(ref, heads_block, store):
+    depth, width = heads_block.shape
+    for j in range(ref.shape[1] // depth):
+        store(
+            slice(j * width, (j + 1) * width),
+            dot(ref[:, j * depth : (j + 1) * depth], heads_block),
+        )
 
 
 def same_head(width, head):
@@ -87,13 +92,12 @@
     return [(c, e) for c in range(positions) for e in range(c + 1)]
 
 
-def depth_body(
-    place_ref, att_ref, emb_ref, codes_ref, gain_ref, w_in_hbm, table_hbm,
-    near_hbm, far_hbm, near_twin_hbm, far_twin_hbm, keep_ref, send_ref,
-    w_in_ref, table_ref, w_ref, w_out_ref, x_ref, n_ref, n_t_ref, qkv_ref, term_ref, s_ref, p_ref, mix_ref, mix_t_ref, inv_ref,
-    logit_ref, g_ref, dr_ref, dqkv_ref, stage_ref, sems, in_sems, table_sem,
-    *, weight, head,
-):
+def depth_body(*refs, weight, head):
+    place_ref, att_ref, codes_ref, gain_ref, emb_hbm, w_in_hbm, table_hbm = refs[:7]
+    shards = refs[7:-26]
+    keep_ref, send_ref, emb_ref, w_in_ref, table_ref, w_ref, w_out_ref, x_ref, n_ref = refs[-26:-17]
+    n_t_ref, qkv_ref, term_ref, s_ref, p_ref, mix_ref, mix_t_ref, inv_ref = refs[-17:-9]
+    logit_ref, g_ref, dr_ref, dqkv_ref, stage_ref, sems, in_sems, emb_sem, table_sem = refs[-9:]
     frames, positions = codes_ref.shape
     width = x_ref.shape[1]
     entries = table_ref.shape[0]
@@ -112,21 +116,24 @@
     load_in = lambda j: pltpu.make_async_copy(
         w_in_hbm.at[:, tile_cols(j)], w_in_ref.at[:, tile_cols(j)], in_sems.at[j]
     )
+    load_emb = pltpu.make_async_copy(emb_hbm, emb_ref, emb_sem)
     load_table = pltpu.make_async_copy(table_hbm, table_ref, table_sem)
-    for j in range(width // tile):
+    load_in(0).start()
+    load_emb.start()
+    for j in range(1, width // tile):
         load_in(j).start()
     loads = []
-    ring = near_hbm.shape[0]
-    quarters = ((0, 0, near_hbm), (0, 1, far_hbm), (1, 0, near_twin_hbm), (1, 1, far_twin_hbm))
-    for twin, plane, ref in quarters:
-        for back in range(ring):
-            at = (place_ref[0] + plane) % 2
-            at = at * ring + (place_ref[1] + ring - back) % ring
-            at = at * 2 + (side + twin) % 2
-            rows = pl.ds(pl.multiple_of(at * rows_qkv, rows_qkv), rows_qkv)
-            loads.append(pltpu.make_async_copy(ref.at[back], w_ref.at[rows], sems.at[len(loads)]))
-            loads[-1].start()
+    ring = len(shards) // 4
+    for k, ref in enumerate(shards):
+        twin, plane, back = k // (2 * ring), k // ring % 2, k % ring
+        at = (place_ref[0] + plane) % 2
+        at = at * ring + (place_ref[1] + ring - back) % ring
+        at = at * 2 + (side + twin) % 2
+        rows = pl.ds(pl.multiple_of(at * rows_qkv, rows_qkv), rows_qkv)
+        loads.append(pltpu.make_async_copy(ref, w_ref.at[rows], sems.at[k]))
+        loads[-1].start()
     load_table.start()
+    load_emb.wait()
     att = jnp.concatenate([att_ref[h] for h in range(att_ref.shape[0])], axis=1)
 
     @pl.loop(0, width // tile)
@@ -158,19 +165,18 @@
         cols = pl.ds(pl.multiple_of(j * tile, tile), tile)
         qkv_ref[:, cols] = dot(n_ref[...], w_ref[:, cols]).astype(bf16)
 
-    block = same_head(tile, head)
+    block = jnp.concatenate([same_head(tile, head)] * 2, axis=0)
     scale = 1.0 / math.sqrt(head)
     pairs = pairs_of(positions)
     part = lambda c, k: qkv_ref[row(c), k * dh : (k + 1) * dh].astype(f32)
-    count = len(pairs)
     pair = lambda c, e: pl.ds(pairs.index((c, e)) * frames, frames)
 
     def store_scores(cols, values):
         s_ref[:, cols] = values * scale
 
-    for k, (c, e) in enumerate(pairs):
-        put_split(term_ref, k, frames, count, part(c, 0) * part(e, 1))
-    head_sums(term_ref, count * frames, block, store_scores)
+    for c, e in pairs:
+        put_split(term_ref, pair(c, e), part(c, 0) * part(e, 1), tile)
+    head_sums(term_ref, block, store_scores)
     for c in range(positions):
         scores = [s_ref[pair(c, e), :] for e in range(c + 1)]
         top = functools.reduce(jnp.maximum, scores)
@@ -240,9 +246,9 @@
     def store_plain(cols, values):
         s_ref[:, cols] = values
 
-    for k, (c, e) in enumerate(pairs):
-        put_split(term_ref, k, frames, count, dmix_ref[row(c), :] * part(e, 2))
-    head_sums(term_ref, count * frames, block, store_plain)
+    for c, e in pairs:
+        put_split(term_ref, pair(c, e), dmix_ref[row(c), :] * part(e, 2), tile)
+    head_sums(term_ref, block, store_plain)
     dk = [jnp.zeros((frames, dh), f32) for _ in range(positions)]
     dv = [jnp.zeros((frames, dh), f32) for _ in range(positions)]
     for c in range(positions):
@@ -370,9 +376,9 @@
 def depth_call(weight, place, attended, embedded, codes, gain, w_in, table, weights):
     frames, positions = codes.shape
     width, entries, rows = w_in.shape[1], table.shape[0], frames * positions
-    dh = (weights[0].shape[2] - width // 2) // 3
-    ring, share, columns = weights[0].shape
-    owners = 2 * ring
+    dh = (weights[0].shape[1] - width // 2) // 3
+    share, columns = weights[0].shape
+    owners = len(weights) // 2
     cut = shape((owners, share, columns))
     pairs = len(pairs_of(positions)) * frames
     return kernel(
@@ -380,9 +386,10 @@
         (cut, cut),
         "depth",
         11 * 10**9,
-        room=44 << 20,
-        in_specs=[SMEM] + [VMEM] * 4 + [HBM] * 6,
+        room=42 << 20,
+        in_specs=[SMEM] + [VMEM] * 3 + [HBM] * (3 + len(weights)),
         scratch=[
+            pltpu.VMEM(embedded.shape, bf16),
             pltpu.VMEM(w_in.shape, bf16),
             pltpu.VMEM(table.shape, bf16),
             pltpu.VMEM((width, columns), bf16),
@@ -391,7 +398,7 @@
             pltpu.VMEM((rows, width), bf16),
             pltpu.VMEM((width, rows), bf16),
             pltpu.VMEM((rows, 3 * dh), bf16),
-            pltpu.VMEM((2 * pairs, dh), bf16),
+            pltpu.VMEM((pairs, 2 * dh), bf16),
             pltpu.VMEM((pairs, dh), f32),
             pltpu.VMEM((pairs, dh), f32),
             pltpu.VMEM((rows, dh), bf16),
@@ -405,8 +412,9 @@
             pltpu.SemaphoreType.DMA((2 * owners,)),
             pltpu.SemaphoreType.DMA((width // 256,)),
             pltpu.SemaphoreType.DMA,
+            pltpu.SemaphoreType.DMA,
         ],
-    )(place, attended, embedded, codes, gain.reshape(1, width), w_in, table, *weights)
+    )(place, attended, codes, gain.reshape(1, width), embedded, w_in, table, *weights)
 
 
 def local(query, keys, values, codes, w_in, table, gain, w_qkv, w_out):
@@ -435,12 +443,6 @@
     both = jnp.concatenate(
         [w_qkv, jnp.concatenate([w_out[:, : width // 2], w_out[:, width // 2 :]], axis=0)], axis=1
     )
-    ring = lax.axis_size("dp_1")
-    planes = [[w] + [turned(w, "dp_1", k) for k in range(1, ring)] for w in (both, turned(both, "dp_0", 1))]
-    weights = [jnp.stack(plane) for plane in planes]
-    weights += [turned(w, "dp_2", 1) for w in weights]
-
-    moved = to_all(packed, CTX)
     embedded = kernel(
         embed_body,
         shape((positions - 1, frames, width)),
@@ -449,6 +451,13 @@
         room=10 << 20,
         scratch=[pltpu.VMEM(((positions - 1) * frames, entries), bf16)],
     )(codes[0], table)
+    other, embedded = lax.optimization_barrier((turned(both, "dp_0", 1), embedded))
+    ring = lax.axis_size("dp_1")
+    weights = [w if k == 0 else turned(w, "dp_1", k) for w in (both, other) for k in range(ring)]
+    weights += [turned(w, "dp_2", 1) for w in weights]
+
+    moved = to_all(packed, CTX)
+    moved, embedded, weights, place = lax.optimization_barrier((moved, embedded, weights, place))
 
     heads = kernel(
         functools.partial(attend_body, step=2),

time: 173 us -> 172 us (level)
  blocking collectives: 60 us -> 81.7 us
  waiting for transfers between devices: 43.2 us -> 25.4 us
  starting transfers between devices: 26.7 us -> 22.3 us
    all_to_all x3 -> x4, blocking collectives: 60 us -> 81.7 us  [to_all(): return lax.all_to_all(x, axis, 0, 0, tiled=True)]
    all_to_all x2 -> x1, waiting for transfers between devices: 20.2 us -> 3.92 us  [to_all(): return lax.all_to_all(x, axis, 0, 0, tiled=True)]
    all_to_all x2 -> x1, starting transfers between devices: 16.6 us -> 11.2 us  [to_all(): return lax.all_to_all(x, axis, 0, 0, tiled=True)]
    unnamed x11 -> x19, local copies, waits for them, and re-layouts: 2.32 us -> 3.92 us
    ppermute x10 -> x16, waiting for transfers between devices: 23 us -> 21.5 us  [turned(): return lax.ppermute(x, axis, [(i, (i + k) % n) for i in range(n)])]
    ppermute x10 -> x16, starting transfers between devices: 10.1 us -> 11.1 us  [turned(): return lax.ppermute(x, axis, [(i, (i + k) % n) for i in range(n)])]
  transfers between devices with their start and end apart: 12 -> 17, of which waited for: 8 -> 8; matrix products, arithmetic and copies ran while one was open for 1% -> 0% of each run, Pallas kernels for 5% -> 2%
where the time goes in v2:
time: 172 us
  blocking collectives  81.7 us (48%)
  Pallas kernels  37.7 us (22%)
  waiting for transfers between devices  25.4 us (15%)
  starting transfers between devices  22.3 us (13%)
  local copies, waits for them, and re-layouts  3.93 us (2%)
    all_to_all x4, blocking collectives, to_all(): return lax.all_to_all(x, axis, 0, 0, tiled=True)  81.7 us
    pallas_call x8, Pallas kernels, call(): pl.pallas_call(body, out_shape=every if many else outs, in_specs=in_specs...  37.7 us
    ppermute x16, waiting for transfers between devices, turned(): return lax.ppermute(x, axis, [(i, (i + k) % n) for i in range(n)])  21.5 us
    all_to_all x1, starting transfers between devices, to_all(): return lax.all_to_all(x, axis, 0, 0, tiled=True)  11.2 us
    ppermute x16, starting transfers between devices, turned(): return lax.ppermute(x, axis, [(i, (i + k) % n) for i in range(n)])  11.1 us
    unnamed x19, local copies, waits for them, and re-layouts  3.92 us
    all_to_all x1, waiting for transfers between devices, to_all(): return lax.all_to_all(x, axis, 0, 0, tiled=True)  3.92 us
  transfers between devices with their start and end apart: 17, of which 8 were waited for; matrix products, arithmetic and copies ran while one was open for 0% of the time, Pallas kernels for 2%

profile of v2, /device:TPU:32, one launch (start us, length us, event | category | flops | bytes accessed | tf_op | source)
XLA Modules:
  0.0 172.0 jit_solution(9138094069581137538)
XLA Ops:
  0.6 2.4 %pack.1 = bf16[16,3,128,128]{3,2,1,0:T(8,128)(2,1)} custom-call(bf16[1,128,2048]{2,1,0:T(8,128)(2,1)} %query_hbm.1, bf16[1,128,2048]{2,1,0:T(8,128)(2,1)} %keys_hbm.1, bf16[1,128,2048]{2,1,0:T(8,128)(2,1)} %values_hbm.1), custom_call_target="tpu_custom_call" | custom-call | flops 1048576 | bytes 3145728 | tf_op jit(solution)/shard_map/pack/pallas_call | solution.py:345
  3.1 11.2 %all-to-all-start = ((bf16[16,3,128,128]{3,2,1,0:T(8,128)(2,1)}), bf16[16,3,128,128]{3,2,1,0:T(8,128)(2,1)S(1)}, u32[]{:S(2)}, u32[]{:S(2)}) async-start(bf16[16,3,128,128]{3,2,1,0:T(8,128)(2,1)} %pack.1), calls=%async_computation | async-start | bytes 3145728 | tf_op jit(solution)/shard_map/all_to_all | solution.py:368
  15.0 3.0 %collective-permute-start.3 = (bf16[64,2048]{1,0:T(8,128)(2,1)S(1)}, bf16[64,2048]{1,0:T(8,128)(2,1)S(1)}, u32[]{:S(2)}, u32[]{:S(2)}) collective-permute-start(bf16[64,2048]{1,0:T(8,128)(2,1)S(1)} %maximum_maximum_fusion.refs_7_), channel_id=1, source_target_pairs={{0,96},{32,0},{64,32},{96,64},{1,97},{33,1},{65,33},{97,65},{2,98}... | collective-permute-start | bytes 786440 | tf_op jit(solution)/shard_map/ppermute | solution.py:373
  18.6 1.0 collective-permute-start.1
  19.7 2.2 %copy-done = bf16[2048,1024]{1,0:T(8,128)(2,1)S(1)} copy-done((bf16[2048,1024]{1,0:T(8,128)(2,1)S(1)}, bf16[2048,1024]{1,0:T(8,128)(2,1)}, u32[]{:S(2)}) %copy-start) | copy-done | bytes 4194328
  21.9 2.7 %embed.1.refs_4_ = bf16[3,128,1024]{2,1,0:T(8,128)(2,1)S(1)} custom-call(s32[128,4]{1,0:T(8,128)S(1)} %bitcast.7, bf16[2048,1024]{1,0:T(8,128)(2,1)S(1)} %copy-done), custom_call_target="tpu_custom_call" | custom-call | flops 1610612736 | bytes 4982784 | tf_op jit(solution)/shard_map/embed/pallas_call | solution.py:345
  24.6 0.9 copy-done.4
  25.5 1.0 collective-permute-done.refs_11_
  26.5 1.8 %collective-permute-done.3.refs_10_ = bf16[64,2048]{1,0:T(8,128)(2,1)S(1)} collective-permute-done((bf16[64,2048]{1,0:T(8,128)(2,1)S(1)}, bf16[64,2048]{1,0:T(8,128)(2,1)S(1)}, u32[]{:S(2)}, u32[]{:S(2)}) %collective-permute-start.3) | collective-permute-done | bytes 262176 | tf_op jit(solution)/shard_map/ppermute | solution.py:373
  28.8 3.7 %collective-permute-start.6 = (bf16[64,2048]{1,0:T(8,128)(2,1)S(1)}, bf16[64,2048]{1,0:T(8,128)(2,1)}, u32[]{:S(2)}, u32[]{:S(2)}) collective-permute-start(bf16[64,2048]{1,0:T(8,128)(2,1)S(1)} %collective-permute-done.refs_11_), channel_id=1, source_target_pairs={{0,96},{32,0},{64,32},{96,64},{1,97},{33,1},{65,33},{97,65},{2,98}... | collective-permute-start | bytes 786440 | tf_op jit(solution)/shard_map/ppermute | solution.py:373
  32.6 0.9 collective-permute-start.4
  33.4 0.7 copy-done.1
  34.6 9.3 %collective-permute-done.6.refs_14_ = bf16[64,2048]{1,0:T(8,128)(2,1)} collective-permute-done((bf16[64,2048]{1,0:T(8,128)(2,1)S(1)}, bf16[64,2048]{1,0:T(8,128)(2,1)}, u32[]{:S(2)}, u32[]{:S(2)}) %collective-permute-start.6) | collective-permute-done | bytes 262176 | tf_op jit(solution)/shard_map/ppermute | solution.py:373
  44.4 3.2 %collective-permute-done.4.refs_12_ = bf16[64,2048]{1,0:T(8,128)(2,1)} collective-permute-done((bf16[64,2048]{1,0:T(8,128)(2,1)S(1)}, bf16[64,2048]{1,0:T(8,128)(2,1)}, u32[]{:S(2)}, u32[]{:S(2)}) %collective-permute-start.4) | collective-permute-done | bytes 262176 | tf_op jit(solution)/shard_map/ppermute | solution.py:373
  47.7 1.8 %collective-permute-done.12.refs_20_ = bf16[64,2048]{1,0:T(8,128)(2,1)} collective-permute-done((bf16[64,2048]{1,0:T(8,128)(2,1)}, bf16[64,2048]{1,0:T(8,128)(2,1)}, u32[]{:S(2)}, u32[]{:S(2)}) %collective-permute-start.12) | collective-permute-done | bytes 262176 | tf_op jit(solution)/shard_map/ppermute | solution.py:373
  49.4 3.9 %all-to-all-done.x_ref = bf16[16,3,128,128]{3,2,1,0:T(8,128)(2,1)S(1)} async-done(((bf16[16,3,128,128]{3,2,1,0:T(8,128)(2,1)}), bf16[16,3,128,128]{3,2,1,0:T(8,128)(2,1)S(1)}, u32[]{:S(2)}, u32[]{:S(2)}) %all-to-all-start) | async-done | bytes 1572896 | tf_op jit(solution)/shard_map/all_to_all | solution.py:368
  53.4 4.5 %attend.1 = bf16[16,128,128]{2,1,0:T(8,128)(2,1)S(1)} custom-call(bf16[16,3,128,128]{3,2,1,0:T(8,128)(2,1)S(1)} %all-to-all-done.x_ref), custom_call_target="tpu_custom_call" | custom-call | flops 2147483648 | bytes 2097152 | tf_op jit(solution)/shard_map/attend/pallas_call | solution.py:345
  57.9 23.0 %all_to_all.25.refs_1_ = bf16[16,128,128]{2,1,0:T(8,128)(2,1)S(1)} all-to-all(bf16[16,128,128]{2,1,0:T(8,128)(2,1)S(1)} %attend.1), channel_id=1, replica_groups=mesh['dp_0'=2,'dp_1'=4,'dp_2'=2,'ctx_0'=2,'ctx_1'=8] {'ctx_0','ctx_1'}, dimensions={0} | all-to-all | bytes 1048576 | tf_op jit(solution)/shard_map/all_to_all | solution.py:368
  80.9 26.5 %depth.1 = (bf16[8,64,2048]{2,1,0:T(8,128)(2,1)S(1)}, bf16[8,64,2048]{2,1,0:T(8,128)(2,1)S(1)}) custom-call(s32[3]{0:T(128)S(1)} %pad_add_fusion.refs_0_, bf16[16,128,128]{2,1,0:T(8,128)(2,1)S(1)} %all_to_all.25.refs_1_, s32[128,4]{1,0:T(8,128)S(1)} %bitcast.8, f32[1,1024]{1,0:T(1,128)S(1)} %bitcast.9, bf16[3,128,1024]{2,1,0:T(8,128)(2,1)S(1)} %copy-done.5, ...), custom_call_target="tpu_custom_call" | custom-call | flops 11000000512 | bytes 18094092 | tf_op jit(solution)/shard_map/depth/pallas_call | solution.py:345
  107.5 4.1 %collective-permute-done.15.b_ref = bf16[8,64,2048]{2,1,0:T(8,128)(2,1)S(1)} collective-permute-done((bf16[8,64,2048]{2,1,0:T(8,128)(2,1)S(1)}, bf16[8,64,2048]{2,1,0:T(8,128)(2,1)S(1)}, u32[]{:S(2)}, u32[]{:S(2)}) %collective-permute-start.15) | collective-permute-done | bytes 2097184 | tf_op jit(solution)/shard_map/ppermute | solution.py:373
  112.1 32.4 %all_to_all.26.x_ref = bf16[16,64,1024]{2,1,0:T(8,128)(2,1)S(1)} all-to-all(bf16[16,64,1024]{2,1,0:T(8,128)(2,1)S(1)} %bitcast.6), channel_id=1, replica_groups=mesh['dp_0'=2,'dp_1'=4,'dp_2'=2,'ctx_0'=2,'ctx_1'=8] {'dp_0','dp_1','ctx..., dimensions={0} | all-to-all | bytes 4194304 | tf_op jit(solution)/shard_map/all_to_all | solution.py:368
  144.8 11.6 %all_to_all.27.x_ref = bf16[8,64,128]{2,1,0:T(8,128)(2,1)S(1)} all-to-all(bf16[8,64,128]{2,1,0:T(8,128)(2,1)S(1)} %plane_sum.1), channel_id=1, replica_groups=mesh['dp_0'=2,'dp_1'=4,'dp_2'=2,'ctx_0'=2,'ctx_1'=8] {'ctx_1'}, dimensions={0} | all-to-all | bytes 262144 | tf_op jit(solution)/shard_map/all_to_all | solution.py:368
  156.4 14.8 %all_to_all.28.x_ref = bf16[16,64,128]{2,1,0:T(8,128)(2,1)S(1)} all-to-all(bf16[16,64,128]{2,1,0:T(8,128)(2,1)S(1)} %whole_sum.1), channel_id=1, replica_groups=mesh['dp_0'=2,'dp_1'=4,'dp_2'=2,'ctx_0'=2,'ctx_1'=8] {'ctx_0','ctx_1'}, dimensions={0} | all-to-all | bytes 524288 | tf_op jit(solution)/shard_map/all_to_all | solution.py:368
  171.2 0.8 lay_out.1
  (44 shorter events, 4.1 us)
Async XLA Ops:
  3.0 11.2 %copy-start.7 = (bf16[32,1024]{1,0:T(8,128)(2,1)S(1)}, bf16[32,1024]{1,0:T(8,128)(2,1)}, u32[]{:S(2)}) copy-start(bf16[32,1024]{1,0:T(8,128)(2,1)} %param.17) | copy-start | bytes 196612
  3.0 11.2 %copy-start.6 = (bf16[64,1536]{1,0:T(8,128)(2,1)S(1)}, bf16[64,1536]{1,0:T(8,128)(2,1)}, u32[]{:S(2)}) copy-start(bf16[64,1536]{1,0:T(8,128)(2,1)} %param.16) | copy-start | bytes 589828
  3.0 16.6 %copy-start.8 = (s32[1,128,4]{1,2,0:T(4,128)S(1)}, s32[1,128,4]{1,2,0:T(4,128)}, u32[]{:S(2)}) copy-start(s32[1,128,4]{1,2,0:T(4,128)} %param.12) | copy-start | bytes 6148
  3.1 50.3 %all-to-all-start = ((bf16[16,3,128,128]{3,2,1,0:T(8,128)(2,1)}), bf16[16,3,128,128]{3,2,1,0:T(8,128)(2,1)S(1)}, u32[]{:S(2)}, u32[]{:S(2)}) async-start(bf16[16,3,128,128]{3,2,1,0:T(8,128)(2,1)} %pack.1), calls=%async_computation | async-start | bytes 3145728 | tf_op jit(solution)/shard_map/all_to_all | solution.py:368
  14.3 12.2 %collective-permute-start = (bf16[64,2048]{1,0:T(8,128)(2,1)S(1)}, bf16[64,2048]{1,0:T(8,128)(2,1)S(1)}, u32[]{:S(2)}, u32[]{:S(2)}) collective-permute-start(bf16[64,2048]{1,0:T(8,128)(2,1)S(1)} %maximum_maximum_fusion.refs_7_), channel_id=1, source_target_pairs={{0,128},{128,0},{1,129},{129,1},{2,130},{130,2},{3,131},{131,3},{4... | collective-permute-start | bytes 786440 | tf_op jit(solution)/shard_map/ppermute | solution.py:373
  15.0 13.4 %collective-permute-start.3 = (bf16[64,2048]{1,0:T(8,128)(2,1)S(1)}, bf16[64,2048]{1,0:T(8,128)(2,1)S(1)}, u32[]{:S(2)}, u32[]{:S(2)}) collective-permute-start(bf16[64,2048]{1,0:T(8,128)(2,1)S(1)} %maximum_maximum_fusion.refs_7_), channel_id=1, source_target_pairs={{0,96},{32,0},{64,32},{96,64},{1,97},{33,1},{65,33},{97,65},{2,98}... | collective-permute-start | bytes 786440 | tf_op jit(solution)/shard_map/ppermute | solution.py:373
  18.0 10.7 %collective-permute-start.2 = (bf16[64,2048]{1,0:T(8,128)(2,1)S(1)}, bf16[64,2048]{1,0:T(8,128)(2,1)S(1)}, u32[]{:S(2)}, u32[]{:S(2)}) collective-permute-start(bf16[64,2048]{1,0:T(8,128)(2,1)S(1)} %maximum_maximum_fusion.refs_7_), channel_id=1, source_target_pairs={{0,64},{32,96},{64,0},{96,32},{1,65},{33,97},{65,1},{97,33},{2,66}... | collective-permute-start | bytes 786440 | tf_op jit(solution)/shard_map/ppermute | solution.py:373
  18.6 13.9 %collective-permute-start.7 = (bf16[64,2048]{1,0:T(8,128)(2,1)S(1)}, bf16[64,2048]{1,0:T(8,128)(2,1)S(1)}, u32[]{:S(2)}, u32[]{:S(2)}) collective-permute-start(bf16[64,2048]{1,0:T(8,128)(2,1)S(1)} %maximum_maximum_fusion.refs_7_), channel_id=1, source_target_pairs={{0,16},{16,0},{1,17},{17,1},{2,18},{18,2},{3,19},{19,3},{4,20},{20... | collective-permute-start | bytes 786440 | tf_op jit(solution)/shard_map/ppermute | solution.py:373
  18.6 13.9 %collective-permute-start.1 = (bf16[64,2048]{1,0:T(8,128)(2,1)S(1)}, bf16[64,2048]{1,0:T(8,128)(2,1)S(1)}, u32[]{:S(2)}, u32[]{:S(2)}) collective-permute-start(bf16[64,2048]{1,0:T(8,128)(2,1)S(1)} %maximum_maximum_fusion.refs_7_), channel_id=1, source_target_pairs={{0,32},{32,64},{64,96},{96,0},{1,33},{33,65},{65,97},{97,1},{2,34}... | collective-permute-start | bytes 786440 | tf_op jit(solution)/shard_map/ppermute | solution.py:373
  19.7 2.2 %copy-start = (bf16[2048,1024]{1,0:T(8,128)(2,1)S(1)}, bf16[2048,1024]{1,0:T(8,128)(2,1)}, u32[]{:S(2)}) copy-start(bf16[2048,1024]{1,0:T(8,128)(2,1)} %refs_6_.1) | copy-start | bytes 12582916
  28.3 5.1 %collective-permute-start.10 = (bf16[64,2048]{1,0:T(8,128)(2,1)S(1)}, bf16[64,2048]{1,0:T(8,128)(2,1)S(1)}, u32[]{:S(2)}, u32[]{:S(2)}) collective-permute-start(bf16[64,2048]{1,0:T(8,128)(2,1)S(1)} %collective-permute-done.3.refs_10_), channel_id=1, source_target_pairs={{0,16},{16,0},{1,17},{17,1},{2,18},{18,2},{3,19},{19,3},{4,20},{20... | collective-permute-start | bytes 786440 | tf_op jit(solution)/shard_map/ppermute | solution.py:373
  28.7 4.7 %collective-permute-start.9 = (bf16[64,2048]{1,0:T(8,128)(2,1)S(1)}, bf16[64,2048]{1,0:T(8,128)(2,1)S(1)}, u32[]{:S(2)}, u32[]{:S(2)}) collective-permute-start(bf16[64,2048]{1,0:T(8,128)(2,1)S(1)} %collective-permute-done.2.refs_9_), channel_id=1, source_target_pairs={{0,16},{16,0},{1,17},{17,1},{2,18},{18,2},{3,19},{19,3},{4,20},{20... | collective-permute-start | bytes 786440 | tf_op jit(solution)/shard_map/ppermute | solution.py:373
  28.8 15.0 %collective-permute-start.6 = (bf16[64,2048]{1,0:T(8,128)(2,1)S(1)}, bf16[64,2048]{1,0:T(8,128)(2,1)}, u32[]{:S(2)}, u32[]{:S(2)}) collective-permute-start(bf16[64,2048]{1,0:T(8,128)(2,1)S(1)} %collective-permute-done.refs_11_), channel_id=1, source_target_pairs={{0,96},{32,0},{64,32},{96,64},{1,97},{33,1},{65,33},{97,65},{2,98}... | collective-permute-start | bytes 786440 | tf_op jit(solution)/shard_map/ppermute | solution.py:373
  32.5 11.4 %collective-permute-start.5 = (bf16[64,2048]{1,0:T(8,128)(2,1)S(1)}, bf16[64,2048]{1,0:T(8,128)(2,1)}, u32[]{:S(2)}, u32[]{:S(2)}) collective-permute-start(bf16[64,2048]{1,0:T(8,128)(2,1)S(1)} %collective-permute-done.refs_11_), channel_id=1, source_target_pairs={{0,64},{32,96},{64,0},{96,32},{1,65},{33,97},{65,1},{97,33},{2,66}... | collective-permute-start | bytes 786440 | tf_op jit(solution)/shard_map/ppermute | solution.py:373
  32.6 15.0 %collective-permute-start.4 = (bf16[64,2048]{1,0:T(8,128)(2,1)S(1)}, bf16[64,2048]{1,0:T(8,128)(2,1)}, u32[]{:S(2)}, u32[]{:S(2)}) collective-permute-start(bf16[64,2048]{1,0:T(8,128)(2,1)S(1)} %collective-permute-done.refs_11_), channel_id=1, source_target_pairs={{0,32},{32,64},{64,96},{96,0},{1,33},{33,65},{65,97},{97,1},{2,34}... | collective-permute-start | bytes 786440 | tf_op jit(solution)/shard_map/ppermute | solution.py:373
  33.4 14.2 %collective-permute-start.11 = (bf16[64,2048]{1,0:T(8,128)(2,1)S(1)}, bf16[64,2048]{1,0:T(8,128)(2,1)}, u32[]{:S(2)}, u32[]{:S(2)}) collective-permute-start(bf16[64,2048]{1,0:T(8,128)(2,1)S(1)} %collective-permute-done.refs_11_), channel_id=1, source_target_pairs={{0,16},{16,0},{1,17},{17,1},{2,18},{18,2},{3,19},{19,3},{4,20},{20... | collective-permute-start | bytes 786440 | tf_op jit(solution)/shard_map/ppermute | solution.py:373
  34.1 13.5 %collective-permute-start.8 = (bf16[64,2048]{1,0:T(8,128)(2,1)S(1)}, bf16[64,2048]{1,0:T(8,128)(2,1)}, u32[]{:S(2)}, u32[]{:S(2)}) collective-permute-start(bf16[64,2048]{1,0:T(8,128)(2,1)S(1)} %collective-permute-done.1.refs_8_), channel_id=1, source_target_pairs={{0,16},{16,0},{1,17},{17,1},{2,18},{18,2},{3,19},{19,3},{4,20},{20... | collective-permute-start | bytes 786440 | tf_op jit(solution)/shard_map/ppermute | solution.py:373
  43.9 3.8 %collective-permute-start.14 = (bf16[64,2048]{1,0:T(8,128)(2,1)}, bf16[64,2048]{1,0:T(8,128)(2,1)}, u32[]{:S(2)}, u32[]{:S(2)}) collective-permute-start(bf16[64,2048]{1,0:T(8,128)(2,1)} %collective-permute-done.6.refs_14_), channel_id=1, source_target_pairs={{0,16},{16,0},{1,17},{17,1},{2,18},{18,2},{3,19},{19,3},{4,20},{20... | collective-permute-start | bytes 786440 | tf_op jit(solution)/shard_map/ppermute | solution.py:373
  43.9 3.8 %collective-permute-start.13 = (bf16[64,2048]{1,0:T(8,128)(2,1)}, bf16[64,2048]{1,0:T(8,128)(2,1)}, u32[]{:S(2)}, u32[]{:S(2)}) collective-permute-start(bf16[64,2048]{1,0:T(8,128)(2,1)} %collective-permute-done.5.refs_13_), channel_id=1, source_target_pairs={{0,16},{16,0},{1,17},{17,1},{2,18},{18,2},{3,19},{19,3},{4,20},{20... | collective-permute-start | bytes 786440 | tf_op jit(solution)/shard_map/ppermute | solution.py:373
  47.6 1.9 %collective-permute-start.12 = (bf16[64,2048]{1,0:T(8,128)(2,1)}, bf16[64,2048]{1,0:T(8,128)(2,1)}, u32[]{:S(2)}, u32[]{:S(2)}) collective-permute-start(bf16[64,2048]{1,0:T(8,128)(2,1)} %collective-permute-done.4.refs_12_), channel_id=1, source_target_pairs={{0,16},{16,0},{1,17},{17,1},{2,18},{18,2},{3,19},{19,3},{4,20},{20... | collective-permute-start | bytes 786440 | tf_op jit(solution)/shard_map/ppermute | solution.py:373
  47.6 33.2 %copy-start.3 = (f32[1024]{0:T(1024)S(1)}, f32[1024]{0:T(1024)}, u32[]{:S(2)}) copy-start(f32[1024]{0:T(1024)} %param.15) | copy-start | bytes 12292
  53.4 27.5 %copy-start.2 = (bf16[64,2048]{1,0:T(8,128)(2,1)S(1)}, bf16[64,2048]{1,0:T(8,128)(2,1)}, u32[]{:S(2)}) copy-start(bf16[64,2048]{1,0:T(8,128)(2,1)} %copy-done.1) | copy-start | bytes 786436
  53.4 27.5 %copy-start.5 = (bf16[3,128,1024]{2,1,0:T(8,128)(2,1)S(1)}, bf16[3,128,1024]{2,1,0:T(8,128)(2,1)}, u32[]{:S(2)}) copy-start(bf16[3,128,1024]{2,1,0:T(8,128)(2,1)} %copy-done.4) | copy-start | bytes 2359300
  107.4 4.2 %collective-permute-start.15 = (bf16[8,64,2048]{2,1,0:T(8,128)(2,1)S(1)}, bf16[8,64,2048]{2,1,0:T(8,128)(2,1)S(1)}, u32[]{:S(2)}, u32[]{:S(2)}) collective-permute-start(bf16[8,64,2048]{2,1,0:T(8,128)(2,1)S(1)} %get-tuple-element.53), channel_id=1, source_target_pairs={{0,16},{16,0},{1,17},{17,1},{2,18},{18,2},{3,19},{19,3},{4,20},{20... | collective-permute-start | bytes 6291464 | tf_op jit(solution)/shard_map/ppermute | solution.py:373
  (2 other events, 1.6 us)

commit v3 on v2

--- a/solution.py
+++ b/solution.py
@@ -131,15 +131,16 @@
         at = at * 2 + (side + twin) % 2
         rows = pl.ds(pl.multiple_of(at * rows_qkv, rows_qkv), rows_qkv)
         loads.append(pltpu.make_async_copy(ref, w_ref.at[rows], sems.at[k]))
-        loads[-1].start()
-    load_table.start()
     load_emb.wait()
+    for j in range(width // tile):
+        load_in(j).wait()
+    for load in loads:
+        load.start()
     att = jnp.concatenate([att_ref[h] for h in range(att_ref.shape[0])], axis=1)
 
-    @pl.loop(0, width // tile)
-    def _(j):
-        cols = pl.ds(pl.multiple_of(j * tile, tile), tile)
-        load_in(j).wait()
+    @pl.loop(0, width // tile, unroll=4)
+    def _(j):
+        cols = pl.ds(pl.multiple_of(j * tile, tile), tile)
         hidden = dot(att, w_in_ref[:, cols])
         x_ref[row(0), cols] = hidden
         for c in range(1, positions):
@@ -154,13 +155,14 @@
 
     for load in loads:
         load.wait()
+    load_table.start()
     for d in range(2 * owners):
         for k in range(2):
             w_out_ref[d * rows_out : (d + 1) * rows_out, k * half : (k + 1) * half] = w_ref[
                 d * rows_qkv + k * rows_out : d * rows_qkv + (k + 1) * rows_out, 3 * dh :
             ]
 
-    @pl.loop(0, 3 * dh // tile)
+    @pl.loop(0, 3 * dh // tile, unroll=6)
     def _(j):
         cols = pl.ds(pl.multiple_of(j * tile, tile), tile)
         qkv_ref[:, cols] = dot(n_ref[...], w_ref[:, cols]).astype(bf16)
@@ -191,7 +193,7 @@
         mix_ref[row(c), :] = mixed
         mix_t_ref[:, row(c)] = mixed.T
 
-    @pl.loop(0, width // tile)
+    @pl.loop(0, width // tile, unroll=4)
     def _(j):
         cols = pl.ds(pl.multiple_of(j * tile, tile), tile)
         z_ref[:, cols] = x_ref[:, cols] + dot(mix_ref[...], w_out_ref[:, cols])
@@ -206,7 +208,7 @@
 
     load_table.wait()
 
-    @pl.loop(0, entries // tile)
+    @pl.loop(0, entries // tile, unroll=8)
     def _(j):
         cols = pl.ds(pl.multiple_of(j * tile, tile), tile)
         logit_ref[:, cols] = dot_nt(dr_ref[...], table_ref[cols, :])
@@ -219,7 +221,7 @@
         hit = jnp.where(ids == codes_ref[:, c : c + 1], weight, 0.0)
         g_ref[row(c), :] = (e * (weight / total) - hit).astype(bf16)
 
-    @pl.loop(0, width // tile)
+    @pl.loop(0, width // tile, unroll=4)
     def _(j):
         cols = pl.ds(pl.multiple_of(j * tile, tile), tile)
         dz_ref[:, cols] = dot(g_ref[...], table_ref[:, cols])
@@ -238,7 +240,7 @@
         keep_ref[:, rows, cols] = stage_ref[:, side, 0:rows_out, :]
         send_ref[:, rows, cols] = stage_ref[:, 1 - side, 0:rows_out, :]
 
-    @pl.loop(0, dh // tile)
+    @pl.loop(0, dh // tile, unroll=2)
     def _(j):
         cols = pl.ds(pl.multiple_of(j * tile, tile), tile)
         dmix_ref[:, cols] = dot_nt(dr_ref[...], w_out_ref[cols, :])
@@ -268,7 +270,7 @@
         dqkv_ref[row(c), dh : 2 * dh] = dk[c].astype(bf16)
         dqkv_ref[row(c), 2 * dh :] = dv[c].astype(bf16)
 
-    @pl.loop(0, 3 * dh // tile)
+    @pl.loop(0, 3 * dh // tile, unroll=6)
     def _(j):
         cols = pl.ds(pl.multiple_of(j * tile, tile), tile)
         part_qkv = dot(n_t_ref[...], dqkv_ref[:, cols]).astype(bf16)

time: 172 us -> 166 us (0.965)
  Pallas kernels: 37.7 us -> 31.4 us
    pallas_call x8, Pallas kernels: 37.7 us -> 31.4 us  [call(): pl.pallas_call(body, out_shape=every if many else outs, in_specs=in_specs...]
where the time goes in v3:
time: 166 us
  blocking collectives  81.7 us (49%)
  Pallas kernels  31.4 us (19%)
  waiting for transfers between devices  25.4 us (15%)
  starting transfers between devices  22.3 us (13%)
  local copies, waits for them, and re-layouts  3.93 us (2%)
    all_to_all x4, blocking collectives, to_all(): return lax.all_to_all(x, axis, 0, 0, tiled=True)  81.7 us
    pallas_call x8, Pallas kernels, call(): pl.pallas_call(body, out_shape=every if many else outs, in_specs=in_specs...  31.4 us
    ppermute x16, waiting for transfers between devices, turned(): return lax.ppermute(x, axis, [(i, (i + k) % n) for i in range(n)])  21.5 us
    all_to_all x1, starting transfers between devices, to_all(): return lax.all_to_all(x, axis, 0, 0, tiled=True)  11.2 us
    ppermute x16, starting transfers between devices, turned(): return lax.ppermute(x, axis, [(i, (i + k) % n) for i in range(n)])  11.1 us
    unnamed x19, local copies, waits for them, and re-layouts  3.92 us
    all_to_all x1, waiting for transfers between devices, to_all(): return lax.all_to_all(x, axis, 0, 0, tiled=True)  3.92 us
  transfers between devices with their start and end apart: 17, of which 8 were waited for; matrix products, arithmetic and copies ran while one was open for 0% of the time, Pallas kernels for 2%

profile of v3, /device:TPU:32, one launch (start us, length us, event | category | flops | bytes accessed | tf_op | source)
XLA Modules:
  0.0 165.7 jit_solution(13092803224229612427)
XLA Ops:
  0.6 2.4 %pack.1 = bf16[16,3,128,128]{3,2,1,0:T(8,128)(2,1)} custom-call(bf16[1,128,2048]{2,1,0:T(8,128)(2,1)} %query_hbm.1, bf16[1,128,2048]{2,1,0:T(8,128)(2,1)} %keys_hbm.1, bf16[1,128,2048]{2,1,0:T(8,128)(2,1)} %values_hbm.1), custom_call_target="tpu_custom_call" | custom-call | flops 1048576 | bytes 3145728 | tf_op jit(solution)/shard_map/pack/pallas_call | solution.py:347
  3.1 11.2 %all-to-all-start = ((bf16[16,3,128,128]{3,2,1,0:T(8,128)(2,1)}), bf16[16,3,128,128]{3,2,1,0:T(8,128)(2,1)S(1)}, u32[]{:S(2)}, u32[]{:S(2)}) async-start(bf16[16,3,128,128]{3,2,1,0:T(8,128)(2,1)} %pack.1), calls=%async_computation | async-start | bytes 3145728 | tf_op jit(solution)/shard_map/all_to_all | solution.py:370
  15.0 3.0 %collective-permute-start.3 = (bf16[64,2048]{1,0:T(8,128)(2,1)S(1)}, bf16[64,2048]{1,0:T(8,128)(2,1)S(1)}, u32[]{:S(2)}, u32[]{:S(2)}) collective-permute-start(bf16[64,2048]{1,0:T(8,128)(2,1)S(1)} %maximum_maximum_fusion.refs_7_), channel_id=1, source_target_pairs={{0,96},{32,0},{64,32},{96,64},{1,97},{33,1},{65,33},{97,65},{2,98}... | collective-permute-start | bytes 786440 | tf_op jit(solution)/shard_map/ppermute | solution.py:375
  18.6 1.0 collective-permute-start.1
  19.7 2.2 %copy-done = bf16[2048,1024]{1,0:T(8,128)(2,1)S(1)} copy-done((bf16[2048,1024]{1,0:T(8,128)(2,1)S(1)}, bf16[2048,1024]{1,0:T(8,128)(2,1)}, u32[]{:S(2)}) %copy-start) | copy-done | bytes 4194328
  21.9 2.7 %embed.1.refs_4_ = bf16[3,128,1024]{2,1,0:T(8,128)(2,1)S(1)} custom-call(s32[128,4]{1,0:T(8,128)S(1)} %bitcast.7, bf16[2048,1024]{1,0:T(8,128)(2,1)S(1)} %copy-done), custom_call_target="tpu_custom_call" | custom-call | flops 1610612736 | bytes 4982784 | tf_op jit(solution)/shard_map/embed/pallas_call | solution.py:347
  24.6 0.9 copy-done.4
  25.5 1.0 collective-permute-done.refs_11_
  26.5 1.8 %collective-permute-done.3.refs_10_ = bf16[64,2048]{1,0:T(8,128)(2,1)S(1)} collective-permute-done((bf16[64,2048]{1,0:T(8,128)(2,1)S(1)}, bf16[64,2048]{1,0:T(8,128)(2,1)S(1)}, u32[]{:S(2)}, u32[]{:S(2)}) %collective-permute-start.3) | collective-permute-done | bytes 262176 | tf_op jit(solution)/shard_map/ppermute | solution.py:375
  28.8 3.7 %collective-permute-start.6 = (bf16[64,2048]{1,0:T(8,128)(2,1)S(1)}, bf16[64,2048]{1,0:T(8,128)(2,1)}, u32[]{:S(2)}, u32[]{:S(2)}) collective-permute-start(bf16[64,2048]{1,0:T(8,128)(2,1)S(1)} %collective-permute-done.refs_11_), channel_id=1, source_target_pairs={{0,96},{32,0},{64,32},{96,64},{1,97},{33,1},{65,33},{97,65},{2,98}... | collective-permute-start | bytes 786440 | tf_op jit(solution)/shard_map/ppermute | solution.py:375
  32.6 0.9 collective-permute-start.4
  33.4 0.7 copy-done.1
  34.6 9.3 %collective-permute-done.6.refs_14_ = bf16[64,2048]{1,0:T(8,128)(2,1)} collective-permute-done((bf16[64,2048]{1,0:T(8,128)(2,1)S(1)}, bf16[64,2048]{1,0:T(8,128)(2,1)}, u32[]{:S(2)}, u32[]{:S(2)}) %collective-permute-start.6) | collective-permute-done | bytes 262176 | tf_op jit(solution)/shard_map/ppermute | solution.py:375
  44.4 3.2 %collective-permute-done.4.refs_12_ = bf16[64,2048]{1,0:T(8,128)(2,1)} collective-permute-done((bf16[64,2048]{1,0:T(8,128)(2,1)S(1)}, bf16[64,2048]{1,0:T(8,128)(2,1)}, u32[]{:S(2)}, u32[]{:S(2)}) %collective-permute-start.4) | collective-permute-done | bytes 262176 | tf_op jit(solution)/shard_map/ppermute | solution.py:375
  47.7 1.8 %collective-permute-done.12.refs_20_ = bf16[64,2048]{1,0:T(8,128)(2,1)} collective-permute-done((bf16[64,2048]{1,0:T(8,128)(2,1)}, bf16[64,2048]{1,0:T(8,128)(2,1)}, u32[]{:S(2)}, u32[]{:S(2)}) %collective-permute-start.12) | collective-permute-done | bytes 262176 | tf_op jit(solution)/shard_map/ppermute | solution.py:375
  49.4 3.9 %all-to-all-done.x_ref = bf16[16,3,128,128]{3,2,1,0:T(8,128)(2,1)S(1)} async-done(((bf16[16,3,128,128]{3,2,1,0:T(8,128)(2,1)}), bf16[16,3,128,128]{3,2,1,0:T(8,128)(2,1)S(1)}, u32[]{:S(2)}, u32[]{:S(2)}) %all-to-all-start) | async-done | bytes 1572896 | tf_op jit(solution)/shard_map/all_to_all | solution.py:370
  53.4 4.5 %attend.1 = bf16[16,128,128]{2,1,0:T(8,128)(2,1)S(1)} custom-call(bf16[16,3,128,128]{3,2,1,0:T(8,128)(2,1)S(1)} %all-to-all-done.x_ref), custom_call_target="tpu_custom_call" | custom-call | flops 2147483648 | bytes 2097152 | tf_op jit(solution)/shard_map/attend/pallas_call | solution.py:347
  57.9 23.0 %all_to_all.25.refs_1_ = bf16[16,128,128]{2,1,0:T(8,128)(2,1)S(1)} all-to-all(bf16[16,128,128]{2,1,0:T(8,128)(2,1)S(1)} %attend.1), channel_id=1, replica_groups=mesh['dp_0'=2,'dp_1'=4,'dp_2'=2,'ctx_0'=2,'ctx_1'=8] {'ctx_0','ctx_1'}, dimensions={0} | all-to-all | bytes 1048576 | tf_op jit(solution)/shard_map/all_to_all | solution.py:370
  80.9 20.2 %depth.1 = (bf16[8,64,2048]{2,1,0:T(8,128)(2,1)S(1)}, bf16[8,64,2048]{2,1,0:T(8,128)(2,1)S(1)}) custom-call(s32[3]{0:T(128)S(1)} %pad_add_fusion.refs_0_, bf16[16,128,128]{2,1,0:T(8,128)(2,1)S(1)} %all_to_all.25.refs_1_, s32[128,4]{1,0:T(8,128)S(1)} %bitcast.8, f32[1,1024]{1,0:T(1,128)S(1)} %bitcast.9, bf16[3,128,1024]{2,1,0:T(8,128)(2,1)S(1)} %copy-done.5, ...), custom_call_target="tpu_custom_call" | custom-call | flops 11000000512 | bytes 18094092 | tf_op jit(solution)/shard_map/depth/pallas_call | solution.py:347
  101.2 4.1 %collective-permute-done.15.b_ref = bf16[8,64,2048]{2,1,0:T(8,128)(2,1)S(1)} collective-permute-done((bf16[8,64,2048]{2,1,0:T(8,128)(2,1)S(1)}, bf16[8,64,2048]{2,1,0:T(8,128)(2,1)S(1)}, u32[]{:S(2)}, u32[]{:S(2)}) %collective-permute-start.15) | collective-permute-done | bytes 2097184 | tf_op jit(solution)/shard_map/ppermute | solution.py:375
  105.8 32.4 %all_to_all.26.x_ref = bf16[16,64,1024]{2,1,0:T(8,128)(2,1)S(1)} all-to-all(bf16[16,64,1024]{2,1,0:T(8,128)(2,1)S(1)} %bitcast.6), channel_id=1, replica_groups=mesh['dp_0'=2,'dp_1'=4,'dp_2'=2,'ctx_0'=2,'ctx_1'=8] {'dp_0','dp_1','ctx..., dimensions={0} | all-to-all | bytes 4194304 | tf_op jit(solution)/shard_map/all_to_all | solution.py:370
  138.5 11.6 %all_to_all.27.x_ref = bf16[8,64,128]{2,1,0:T(8,128)(2,1)S(1)} all-to-all(bf16[8,64,128]{2,1,0:T(8,128)(2,1)S(1)} %plane_sum.1), channel_id=1, replica_groups=mesh['dp_0'=2,'dp_1'=4,'dp_2'=2,'ctx_0'=2,'ctx_1'=8] {'ctx_1'}, dimensions={0} | all-to-all | bytes 262144 | tf_op jit(solution)/shard_map/all_to_all | solution.py:370
  150.1 14.8 %all_to_all.28.x_ref = bf16[16,64,128]{2,1,0:T(8,128)(2,1)S(1)} all-to-all(bf16[16,64,128]{2,1,0:T(8,128)(2,1)S(1)} %whole_sum.1), channel_id=1, replica_groups=mesh['dp_0'=2,'dp_1'=4,'dp_2'=2,'ctx_0'=2,'ctx_1'=8] {'ctx_0','ctx_1'}, dimensions={0} | all-to-all | bytes 524288 | tf_op jit(solution)/shard_map/all_to_all | solution.py:370
  164.9 0.8 lay_out.1
  (44 shorter events, 4.1 us)
Async XLA Ops:
  3.0 11.2 %copy-start.7 = (bf16[32,1024]{1,0:T(8,128)(2,1)S(1)}, bf16[32,1024]{1,0:T(8,128)(2,1)}, u32[]{:S(2)}) copy-start(bf16[32,1024]{1,0:T(8,128)(2,1)} %param.17) | copy-start | bytes 196612
  3.0 11.2 %copy-start.6 = (bf16[64,1536]{1,0:T(8,128)(2,1)S(1)}, bf16[64,1536]{1,0:T(8,128)(2,1)}, u32[]{:S(2)}) copy-start(bf16[64,1536]{1,0:T(8,128)(2,1)} %param.16) | copy-start | bytes 589828
  3.0 16.6 %copy-start.8 = (s32[1,128,4]{1,2,0:T(4,128)S(1)}, s32[1,128,4]{1,2,0:T(4,128)}, u32[]{:S(2)}) copy-start(s32[1,128,4]{1,2,0:T(4,128)} %param.12) | copy-start | bytes 6148
  3.1 50.3 %all-to-all-start = ((bf16[16,3,128,128]{3,2,1,0:T(8,128)(2,1)}), bf16[16,3,128,128]{3,2,1,0:T(8,128)(2,1)S(1)}, u32[]{:S(2)}, u32[]{:S(2)}) async-start(bf16[16,3,128,128]{3,2,1,0:T(8,128)(2,1)} %pack.1), calls=%async_computation | async-start | bytes 3145728 | tf_op jit(solution)/shard_map/all_to_all | solution.py:370
  14.3 12.2 %collective-permute-start = (bf16[64,2048]{1,0:T(8,128)(2,1)S(1)}, bf16[64,2048]{1,0:T(8,128)(2,1)S(1)}, u32[]{:S(2)}, u32[]{:S(2)}) collective-permute-start(bf16[64,2048]{1,0:T(8,128)(2,1)S(1)} %maximum_maximum_fusion.refs_7_), channel_id=1, source_target_pairs={{0,128},{128,0},{1,129},{129,1},{2,130},{130,2},{3,131},{131,3},{4... | collective-permute-start | bytes 786440 | tf_op jit(solution)/shard_map/ppermute | solution.py:375
  15.0 13.4 %collective-permute-start.3 = (bf16[64,2048]{1,0:T(8,128)(2,1)S(1)}, bf16[64,2048]{1,0:T(8,128)(2,1)S(1)}, u32[]{:S(2)}, u32[]{:S(2)}) collective-permute-start(bf16[64,2048]{1,0:T(8,128)(2,1)S(1)} %maximum_maximum_fusion.refs_7_), channel_id=1, source_target_pairs={{0,96},{32,0},{64,32},{96,64},{1,97},{33,1},{65,33},{97,65},{2,98}... | collective-permute-start | bytes 786440 | tf_op jit(solution)/shard_map/ppermute | solution.py:375
  18.0 10.7 %collective-permute-start.2 = (bf16[64,2048]{1,0:T(8,128)(2,1)S(1)}, bf16[64,2048]{1,0:T(8,128)(2,1)S(1)}, u32[]{:S(2)}, u32[]{:S(2)}) collective-permute-start(bf16[64,2048]{1,0:T(8,128)(2,1)S(1)} %maximum_maximum_fusion.refs_7_), channel_id=1, source_target_pairs={{0,64},{32,96},{64,0},{96,32},{1,65},{33,97},{65,1},{97,33},{2,66}... | collective-permute-start | bytes 786440 | tf_op jit(solution)/shard_map/ppermute | solution.py:375
  18.6 13.9 %collective-permute-start.7 = (bf16[64,2048]{1,0:T(8,128)(2,1)S(1)}, bf16[64,2048]{1,0:T(8,128)(2,1)S(1)}, u32[]{:S(2)}, u32[]{:S(2)}) collective-permute-start(bf16[64,2048]{1,0:T(8,128)(2,1)S(1)} %maximum_maximum_fusion.refs_7_), channel_id=1, source_target_pairs={{0,16},{16,0},{1,17},{17,1},{2,18},{18,2},{3,19},{19,3},{4,20},{20... | collective-permute-start | bytes 786440 | tf_op jit(solution)/shard_map/ppermute | solution.py:375
  18.6 13.9 %collective-permute-start.1 = (bf16[64,2048]{1,0:T(8,128)(2,1)S(1)}, bf16[64,2048]{1,0:T(8,128)(2,1)S(1)}, u32[]{:S(2)}, u32[]{:S(2)}) collective-permute-start(bf16[64,2048]{1,0:T(8,128)(2,1)S(1)} %maximum_maximum_fusion.refs_7_), channel_id=1, source_target_pairs={{0,32},{32,64},{64,96},{96,0},{1,33},{33,65},{65,97},{97,1},{2,34}... | collective-permute-start | bytes 786440 | tf_op jit(solution)/shard_map/ppermute | solution.py:375
  19.7 2.2 %copy-start = (bf16[2048,1024]{1,0:T(8,128)(2,1)S(1)}, bf16[2048,1024]{1,0:T(8,128)(2,1)}, u32[]{:S(2)}) copy-start(bf16[2048,1024]{1,0:T(8,128)(2,1)} %refs_6_.1) | copy-start | bytes 12582916
  28.3 5.1 %collective-permute-start.10 = (bf16[64,2048]{1,0:T(8,128)(2,1)S(1)}, bf16[64,2048]{1,0:T(8,128)(2,1)S(1)}, u32[]{:S(2)}, u32[]{:S(2)}) collective-permute-start(bf16[64,2048]{1,0:T(8,128)(2,1)S(1)} %collective-permute-done.3.refs_10_), channel_id=1, source_target_pairs={{0,16},{16,0},{1,17},{17,1},{2,18},{18,2},{3,19},{19,3},{4,20},{20... | collective-permute-start | bytes 786440 | tf_op jit(solution)/shard_map/ppermute | solution.py:375
  28.7 4.7 %collective-permute-start.9 = (bf16[64,2048]{1,0:T(8,128)(2,1)S(1)}, bf16[64,2048]{1,0:T(8,128)(2,1)S(1)}, u32[]{:S(2)}, u32[]{:S(2)}) collective-permute-start(bf16[64,2048]{1,0:T(8,128)(2,1)S(1)} %collective-permute-done.2.refs_9_), channel_id=1, source_target_pairs={{0,16},{16,0},{1,17},{17,1},{2,18},{18,2},{3,19},{19,3},{4,20},{20... | collective-permute-start | bytes 786440 | tf_op jit(solution)/shard_map/ppermute | solution.py:375
  28.8 15.0 %collective-permute-start.6 = (bf16[64,2048]{1,0:T(8,128)(2,1)S(1)}, bf16[64,2048]{1,0:T(8,128)(2,1)}, u32[]{:S(2)}, u32[]{:S(2)}) collective-permute-start(bf16[64,2048]{1,0:T(8,128)(2,1)S(1)} %collective-permute-done.refs_11_), channel_id=1, source_target_pairs={{0,96},{32,0},{64,32},{96,64},{1,97},{33,1},{65,33},{97,65},{2,98}... | collective-permute-start | bytes 786440 | tf_op jit(solution)/shard_map/ppermute | solution.py:375
  32.5 11.4 %collective-permute-start.5 = (bf16[64,2048]{1,0:T(8,128)(2,1)S(1)}, bf16[64,2048]{1,0:T(8,128)(2,1)}, u32[]{:S(2)}, u32[]{:S(2)}) collective-permute-start(bf16[64,2048]{1,0:T(8,128)(2,1)S(1)} %collective-permute-done.refs_11_), channel_id=1, source_target_pairs={{0,64},{32,96},{64,0},{96,32},{1,65},{33,97},{65,1},{97,33},{2,66}... | collective-permute-start | bytes 786440 | tf_op jit(solution)/shard_map/ppermute | solution.py:375
  32.6 15.0 %collective-permute-start.4 = (bf16[64,2048]{1,0:T(8,128)(2,1)S(1)}, bf16[64,2048]{1,0:T(8,128)(2,1)}, u32[]{:S(2)}, u32[]{:S(2)}) collective-permute-start(bf16[64,2048]{1,0:T(8,128)(2,1)S(1)} %collective-permute-done.refs_11_), channel_id=1, source_target_pairs={{0,32},{32,64},{64,96},{96,0},{1,33},{33,65},{65,97},{97,1},{2,34}... | collective-permute-start | bytes 786440 | tf_op jit(solution)/shard_map/ppermute | solution.py:375
  33.4 14.2 %collective-permute-start.11 = (bf16[64,2048]{1,0:T(8,128)(2,1)S(1)}, bf16[64,2048]{1,0:T(8,128)(2,1)}, u32[]{:S(2)}, u32[]{:S(2)}) collective-permute-start(bf16[64,2048]{1,0:T(8,128)(2,1)S(1)} %collective-permute-done.refs_11_), channel_id=1, source_target_pairs={{0,16},{16,0},{1,17},{17,1},{2,18},{18,2},{3,19},{19,3},{4,20},{20... | collective-permute-start | bytes 786440 | tf_op jit(solution)/shard_map/ppermute | solution.py:375
  34.1 13.5 %collective-permute-start.8 = (bf16[64,2048]{1,0:T(8,128)(2,1)S(1)}, bf16[64,2048]{1,0:T(8,128)(2,1)}, u32[]{:S(2)}, u32[]{:S(2)}) collective-permute-start(bf16[64,2048]{1,0:T(8,128)(2,1)S(1)} %collective-permute-done.1.refs_8_), channel_id=1, source_target_pairs={{0,16},{16,0},{1,17},{17,1},{2,18},{18,2},{3,19},{19,3},{4,20},{20... | collective-permute-start | bytes 786440 | tf_op jit(solution)/shard_map/ppermute | solution.py:375
  43.9 3.8 %collective-permute-start.14 = (bf16[64,2048]{1,0:T(8,128)(2,1)}, bf16[64,2048]{1,0:T(8,128)(2,1)}, u32[]{:S(2)}, u32[]{:S(2)}) collective-permute-start(bf16[64,2048]{1,0:T(8,128)(2,1)} %collective-permute-done.6.refs_14_), channel_id=1, source_target_pairs={{0,16},{16,0},{1,17},{17,1},{2,18},{18,2},{3,19},{19,3},{4,20},{20... | collective-permute-start | bytes 786440 | tf_op jit(solution)/shard_map/ppermute | solution.py:375
  43.9 3.8 %collective-permute-start.13 = (bf16[64,2048]{1,0:T(8,128)(2,1)}, bf16[64,2048]{1,0:T(8,128)(2,1)}, u32[]{:S(2)}, u32[]{:S(2)}) collective-permute-start(bf16[64,2048]{1,0:T(8,128)(2,1)} %collective-permute-done.5.refs_13_), channel_id=1, source_target_pairs={{0,16},{16,0},{1,17},{17,1},{2,18},{18,2},{3,19},{19,3},{4,20},{20... | collective-permute-start | bytes 786440 | tf_op jit(solution)/shard_map/ppermute | solution.py:375
  47.6 1.9 %collective-permute-start.12 = (bf16[64,2048]{1,0:T(8,128)(2,1)}, bf16[64,2048]{1,0:T(8,128)(2,1)}, u32[]{:S(2)}, u32[]{:S(2)}) collective-permute-start(bf16[64,2048]{1,0:T(8,128)(2,1)} %collective-permute-done.4.refs_12_), channel_id=1, source_target_pairs={{0,16},{16,0},{1,17},{17,1},{2,18},{18,2},{3,19},{19,3},{4,20},{20... | collective-permute-start | bytes 786440 | tf_op jit(solution)/shard_map/ppermute | solution.py:375
  47.6 33.2 %copy-start.3 = (f32[1024]{0:T(1024)S(1)}, f32[1024]{0:T(1024)}, u32[]{:S(2)}) copy-start(f32[1024]{0:T(1024)} %param.15) | copy-start | bytes 12292
  53.4 27.5 %copy-start.2 = (bf16[64,2048]{1,0:T(8,128)(2,1)S(1)}, bf16[64,2048]{1,0:T(8,128)(2,1)}, u32[]{:S(2)}) copy-start(bf16[64,2048]{1,0:T(8,128)(2,1)} %copy-done.1) | copy-start | bytes 786436
  53.4 27.5 %copy-start.5 = (bf16[3,128,1024]{2,1,0:T(8,128)(2,1)S(1)}, bf16[3,128,1024]{2,1,0:T(8,128)(2,1)}, u32[]{:S(2)}) copy-start(bf16[3,128,1024]{2,1,0:T(8,128)(2,1)} %copy-done.4) | copy-start | bytes 2359300
  101.1 4.2 %collective-permute-start.15 = (bf16[8,64,2048]{2,1,0:T(8,128)(2,1)S(1)}, bf16[8,64,2048]{2,1,0:T(8,128)(2,1)S(1)}, u32[]{:S(2)}, u32[]{:S(2)}) collective-permute-start(bf16[8,64,2048]{2,1,0:T(8,128)(2,1)S(1)} %get-tuple-element.53), channel_id=1, source_target_pairs={{0,16},{16,0},{1,17},{17,1},{2,18},{18,2},{3,19},{19,3},{4,20},{20... | collective-permute-start | bytes 6291464 | tf_op jit(solution)/shard_map/ppermute | solution.py:375
  (2 other events, 1.6 us)

commit v4 on v3

--- a/solution.py
+++ b/solution.py
@@ -134,8 +134,9 @@
     load_emb.wait()
     for j in range(width // tile):
         load_in(j).wait()
-    for load in loads:
-        load.start()
+        if j == 1:
+            for load in loads:
+                load.start()
     att = jnp.concatenate([att_ref[h] for h in range(att_ref.shape[0])], axis=1)
 
     @pl.loop(0, width // tile, unroll=4)

time: 166 us -> 165 us (level)
  no operation moved by 1% of the time
where the time goes in v4:
time: 165 us; the launch traced here: 164 us
  blocking collectives  81.7 us (50%)
  Pallas kernels  30.2 us (18%)
  waiting for transfers between devices  25.4 us (15%)
  starting transfers between devices  22.3 us (14%)
  local copies, waits for them, and re-layouts  3.93 us (2%)
    all_to_all x4, blocking collectives, to_all(): return lax.all_to_all(x, axis, 0, 0, tiled=True)  81.7 us
    pallas_call x8, Pallas kernels, call(): pl.pallas_call(body, out_shape=every if many else outs, in_specs=in_specs...  30.2 us
    ppermute x16, waiting for transfers between devices, turned(): return lax.ppermute(x, axis, [(i, (i + k) % n) for i in range(n)])  21.5 us
    all_to_all x1, starting transfers between devices, to_all(): return lax.all_to_all(x, axis, 0, 0, tiled=True)  11.2 us
    ppermute x16, starting transfers between devices, turned(): return lax.ppermute(x, axis, [(i, (i + k) % n) for i in range(n)])  11.1 us
    unnamed x19, local copies, waits for them, and re-layouts  3.92 us
    all_to_all x1, waiting for transfers between devices, to_all(): return lax.all_to_all(x, axis, 0, 0, tiled=True)  3.92 us
  transfers between devices with their start and end apart: 17, of which 8 were waited for; matrix products, arithmetic and copies ran while one was open for 0% of the time, Pallas kernels for 2%

profile of v4, /device:TPU:32, one launch (start us, length us, event | category | flops | bytes accessed | tf_op | source)
XLA Modules:
  0.0 164.4 jit_solution(875255761622534139)
XLA Ops:
  0.6 2.4 %pack.1 = bf16[16,3,128,128]{3,2,1,0:T(8,128)(2,1)} custom-call(bf16[1,128,2048]{2,1,0:T(8,128)(2,1)} %query_hbm.1, bf16[1,128,2048]{2,1,0:T(8,128)(2,1)} %keys_hbm.1, bf16[1,128,2048]{2,1,0:T(8,128)(2,1)} %values_hbm.1), custom_call_target="tpu_custom_call" | custom-call | flops 1048576 | bytes 3145728 | tf_op jit(solution)/shard_map/pack/pallas_call | solution.py:348
  3.1 11.2 %all-to-all-start = ((bf16[16,3,128,128]{3,2,1,0:T(8,128)(2,1)}), bf16[16,3,128,128]{3,2,1,0:T(8,128)(2,1)S(1)}, u32[]{:S(2)}, u32[]{:S(2)}) async-start(bf16[16,3,128,128]{3,2,1,0:T(8,128)(2,1)} %pack.1), calls=%async_computation | async-start | bytes 3145728 | tf_op jit(solution)/shard_map/all_to_all | solution.py:371
  15.0 3.0 %collective-permute-start.3 = (bf16[64,2048]{1,0:T(8,128)(2,1)S(1)}, bf16[64,2048]{1,0:T(8,128)(2,1)S(1)}, u32[]{:S(2)}, u32[]{:S(2)}) collective-permute-start(bf16[64,2048]{1,0:T(8,128)(2,1)S(1)} %maximum_maximum_fusion.refs_7_), channel_id=1, source_target_pairs={{0,96},{32,0},{64,32},{96,64},{1,97},{33,1},{65,33},{97,65},{2,98}... | collective-permute-start | bytes 786440 | tf_op jit(solution)/shard_map/ppermute | solution.py:376
  18.6 1.0 collective-permute-start.1
  19.7 2.2 %copy-done = bf16[2048,1024]{1,0:T(8,128)(2,1)S(1)} copy-done((bf16[2048,1024]{1,0:T(8,128)(2,1)S(1)}, bf16[2048,1024]{1,0:T(8,128)(2,1)}, u32[]{:S(2)}) %copy-start) | copy-done | bytes 4194328
  21.9 2.7 %embed.1.refs_4_ = bf16[3,128,1024]{2,1,0:T(8,128)(2,1)S(1)} custom-call(s32[128,4]{1,0:T(8,128)S(1)} %bitcast.7, bf16[2048,1024]{1,0:T(8,128)(2,1)S(1)} %copy-done), custom_call_target="tpu_custom_call" | custom-call | flops 1610612736 | bytes 4982784 | tf_op jit(solution)/shard_map/embed/pallas_call | solution.py:348
  24.6 0.9 copy-done.4
  25.5 1.0 collective-permute-done.refs_11_
  26.5 1.8 %collective-permute-done.3.refs_10_ = bf16[64,2048]{1,0:T(8,128)(2,1)S(1)} collective-permute-done((bf16[64,2048]{1,0:T(8,128)(2,1)S(1)}, bf16[64,2048]{1,0:T(8,128)(2,1)S(1)}, u32[]{:S(2)}, u32[]{:S(2)}) %collective-permute-start.3) | collective-permute-done | bytes 262176 | tf_op jit(solution)/shard_map/ppermute | solution.py:376
  28.8 3.7 %collective-permute-start.6 = (bf16[64,2048]{1,0:T(8,128)(2,1)S(1)}, bf16[64,2048]{1,0:T(8,128)(2,1)}, u32[]{:S(2)}, u32[]{:S(2)}) collective-permute-start(bf16[64,2048]{1,0:T(8,128)(2,1)S(1)} %collective-permute-done.refs_11_), channel_id=1, source_target_pairs={{0,96},{32,0},{64,32},{96,64},{1,97},{33,1},{65,33},{97,65},{2,98}... | collective-permute-start | bytes 786440 | tf_op jit(solution)/shard_map/ppermute | solution.py:376
  32.6 0.9 collective-permute-start.4
  33.4 0.7 copy-done.1
  34.6 9.3 %collective-permute-done.6.refs_14_ = bf16[64,2048]{1,0:T(8,128)(2,1)} collective-permute-done((bf16[64,2048]{1,0:T(8,128)(2,1)S(1)}, bf16[64,2048]{1,0:T(8,128)(2,1)}, u32[]{:S(2)}, u32[]{:S(2)}) %collective-permute-start.6) | collective-permute-done | bytes 262176 | tf_op jit(solution)/shard_map/ppermute | solution.py:376
  44.4 3.2 %collective-permute-done.4.refs_12_ = bf16[64,2048]{1,0:T(8,128)(2,1)} collective-permute-done((bf16[64,2048]{1,0:T(8,128)(2,1)S(1)}, bf16[64,2048]{1,0:T(8,128)(2,1)}, u32[]{:S(2)}, u32[]{:S(2)}) %collective-permute-start.4) | collective-permute-done | bytes 262176 | tf_op jit(solution)/shard_map/ppermute | solution.py:376
  47.7 1.8 %collective-permute-done.12.refs_20_ = bf16[64,2048]{1,0:T(8,128)(2,1)} collective-permute-done((bf16[64,2048]{1,0:T(8,128)(2,1)}, bf16[64,2048]{1,0:T(8,128)(2,1)}, u32[]{:S(2)}, u32[]{:S(2)}) %collective-permute-start.12) | collective-permute-done | bytes 262176 | tf_op jit(solution)/shard_map/ppermute | solution.py:376
  49.4 3.9 %all-to-all-done.x_ref = bf16[16,3,128,128]{3,2,1,0:T(8,128)(2,1)S(1)} async-done(((bf16[16,3,128,128]{3,2,1,0:T(8,128)(2,1)}), bf16[16,3,128,128]{3,2,1,0:T(8,128)(2,1)S(1)}, u32[]{:S(2)}, u32[]{:S(2)}) %all-to-all-start) | async-done | bytes 1572896 | tf_op jit(solution)/shard_map/all_to_all | solution.py:371
  53.4 4.5 %attend.1 = bf16[16,128,128]{2,1,0:T(8,128)(2,1)S(1)} custom-call(bf16[16,3,128,128]{3,2,1,0:T(8,128)(2,1)S(1)} %all-to-all-done.x_ref), custom_call_target="tpu_custom_call" | custom-call | flops 2147483648 | bytes 2097152 | tf_op jit(solution)/shard_map/attend/pallas_call | solution.py:348
  57.9 23.0 %all_to_all.25.refs_1_ = bf16[16,128,128]{2,1,0:T(8,128)(2,1)S(1)} all-to-all(bf16[16,128,128]{2,1,0:T(8,128)(2,1)S(1)} %attend.1), channel_id=1, replica_groups=mesh['dp_0'=2,'dp_1'=4,'dp_2'=2,'ctx_0'=2,'ctx_1'=8] {'ctx_0','ctx_1'}, dimensions={0} | all-to-all | bytes 1048576 | tf_op jit(solution)/shard_map/all_to_all | solution.py:371
  80.9 18.9 %depth.1 = (bf16[8,64,2048]{2,1,0:T(8,128)(2,1)S(1)}, bf16[8,64,2048]{2,1,0:T(8,128)(2,1)S(1)}) custom-call(s32[3]{0:T(128)S(1)} %pad_add_fusion.refs_0_, bf16[16,128,128]{2,1,0:T(8,128)(2,1)S(1)} %all_to_all.25.refs_1_, s32[128,4]{1,0:T(8,128)S(1)} %bitcast.8, f32[1,1024]{1,0:T(1,128)S(1)} %bitcast.9, bf16[3,128,1024]{2,1,0:T(8,128)(2,1)S(1)} %copy-done.5, ...), custom_call_target="tpu_custom_call" | custom-call | flops 11000000512 | bytes 18094092 | tf_op jit(solution)/shard_map/depth/pallas_call | solution.py:348
  99.9 4.1 %collective-permute-done.15.b_ref = bf16[8,64,2048]{2,1,0:T(8,128)(2,1)S(1)} collective-permute-done((bf16[8,64,2048]{2,1,0:T(8,128)(2,1)S(1)}, bf16[8,64,2048]{2,1,0:T(8,128)(2,1)S(1)}, u32[]{:S(2)}, u32[]{:S(2)}) %collective-permute-start.15) | collective-permute-done | bytes 2097184 | tf_op jit(solution)/shard_map/ppermute | solution.py:376
  104.6 32.3 %all_to_all.26.x_ref = bf16[16,64,1024]{2,1,0:T(8,128)(2,1)S(1)} all-to-all(bf16[16,64,1024]{2,1,0:T(8,128)(2,1)S(1)} %bitcast.6), channel_id=1, replica_groups=mesh['dp_0'=2,'dp_1'=4,'dp_2'=2,'ctx_0'=2,'ctx_1'=8] {'dp_0','dp_1','ctx..., dimensions={0} | all-to-all | bytes 4194304 | tf_op jit(solution)/shard_map/all_to_all | solution.py:371
  137.2 11.6 %all_to_all.27.x_ref = bf16[8,64,128]{2,1,0:T(8,128)(2,1)S(1)} all-to-all(bf16[8,64,128]{2,1,0:T(8,128)(2,1)S(1)} %plane_sum.1), channel_id=1, replica_groups=mesh['dp_0'=2,'dp_1'=4,'dp_2'=2,'ctx_0'=2,'ctx_1'=8] {'ctx_1'}, dimensions={0} | all-to-all | bytes 262144 | tf_op jit(solution)/shard_map/all_to_all | solution.py:371
  148.9 14.7 %all_to_all.28.x_ref = bf16[16,64,128]{2,1,0:T(8,128)(2,1)S(1)} all-to-all(bf16[16,64,128]{2,1,0:T(8,128)(2,1)S(1)} %whole_sum.1), channel_id=1, replica_groups=mesh['dp_0'=2,'dp_1'=4,'dp_2'=2,'ctx_0'=2,'ctx_1'=8] {'ctx_0','ctx_1'}, dimensions={0} | all-to-all | bytes 524288 | tf_op jit(solution)/shard_map/all_to_all | solution.py:371
  163.6 0.8 lay_out.1
  (44 shorter events, 4.1 us)
Async XLA Ops:
  3.0 11.2 %copy-start.7 = (bf16[32,1024]{1,0:T(8,128)(2,1)S(1)}, bf16[32,1024]{1,0:T(8,128)(2,1)}, u32[]{:S(2)}) copy-start(bf16[32,1024]{1,0:T(8,128)(2,1)} %param.17) | copy-start | bytes 196612
  3.0 11.2 %copy-start.6 = (bf16[64,1536]{1,0:T(8,128)(2,1)S(1)}, bf16[64,1536]{1,0:T(8,128)(2,1)}, u32[]{:S(2)}) copy-start(bf16[64,1536]{1,0:T(8,128)(2,1)} %param.16) | copy-start | bytes 589828
  3.0 16.6 %copy-start.8 = (s32[1,128,4]{1,2,0:T(4,128)S(1)}, s32[1,128,4]{1,2,0:T(4,128)}, u32[]{:S(2)}) copy-start(s32[1,128,4]{1,2,0:T(4,128)} %param.12) | copy-start | bytes 6148
  3.1 50.3 %all-to-all-start = ((bf16[16,3,128,128]{3,2,1,0:T(8,128)(2,1)}), bf16[16,3,128,128]{3,2,1,0:T(8,128)(2,1)S(1)}, u32[]{:S(2)}, u32[]{:S(2)}) async-start(bf16[16,3,128,128]{3,2,1,0:T(8,128)(2,1)} %pack.1), calls=%async_computation | async-start | bytes 3145728 | tf_op jit(solution)/shard_map/all_to_all | solution.py:371
  14.3 12.2 %collective-permute-start = (bf16[64,2048]{1,0:T(8,128)(2,1)S(1)}, bf16[64,2048]{1,0:T(8,128)(2,1)S(1)}, u32[]{:S(2)}, u32[]{:S(2)}) collective-permute-start(bf16[64,2048]{1,0:T(8,128)(2,1)S(1)} %maximum_maximum_fusion.refs_7_), channel_id=1, source_target_pairs={{0,128},{128,0},{1,129},{129,1},{2,130},{130,2},{3,131},{131,3},{4... | collective-permute-start | bytes 786440 | tf_op jit(solution)/shard_map/ppermute | solution.py:376
  15.0 13.4 %collective-permute-start.3 = (bf16[64,2048]{1,0:T(8,128)(2,1)S(1)}, bf16[64,2048]{1,0:T(8,128)(2,1)S(1)}, u32[]{:S(2)}, u32[]{:S(2)}) collective-permute-start(bf16[64,2048]{1,0:T(8,128)(2,1)S(1)} %maximum_maximum_fusion.refs_7_), channel_id=1, source_target_pairs={{0,96},{32,0},{64,32},{96,64},{1,97},{33,1},{65,33},{97,65},{2,98}... | collective-permute-start | bytes 786440 | tf_op jit(solution)/shard_map/ppermute | solution.py:376
  18.0 10.7 %collective-permute-start.2 = (bf16[64,2048]{1,0:T(8,128)(2,1)S(1)}, bf16[64,2048]{1,0:T(8,128)(2,1)S(1)}, u32[]{:S(2)}, u32[]{:S(2)}) collective-permute-start(bf16[64,2048]{1,0:T(8,128)(2,1)S(1)} %maximum_maximum_fusion.refs_7_), channel_id=1, source_target_pairs={{0,64},{32,96},{64,0},{96,32},{1,65},{33,97},{65,1},{97,33},{2,66}... | collective-permute-start | bytes 786440 | tf_op jit(solution)/shard_map/ppermute | solution.py:376
  18.6 13.9 %collective-permute-start.7 = (bf16[64,2048]{1,0:T(8,128)(2,1)S(1)}, bf16[64,2048]{1,0:T(8,128)(2,1)S(1)}, u32[]{:S(2)}, u32[]{:S(2)}) collective-permute-start(bf16[64,2048]{1,0:T(8,128)(2,1)S(1)} %maximum_maximum_fusion.refs_7_), channel_id=1, source_target_pairs={{0,16},{16,0},{1,17},{17,1},{2,18},{18,2},{3,19},{19,3},{4,20},{20... | collective-permute-start | bytes 786440 | tf_op jit(solution)/shard_map/ppermute | solution.py:376
  18.6 13.9 %collective-permute-start.1 = (bf16[64,2048]{1,0:T(8,128)(2,1)S(1)}, bf16[64,2048]{1,0:T(8,128)(2,1)S(1)}, u32[]{:S(2)}, u32[]{:S(2)}) collective-permute-start(bf16[64,2048]{1,0:T(8,128)(2,1)S(1)} %maximum_maximum_fusion.refs_7_), channel_id=1, source_target_pairs={{0,32},{32,64},{64,96},{96,0},{1,33},{33,65},{65,97},{97,1},{2,34}... | collective-permute-start | bytes 786440 | tf_op jit(solution)/shard_map/ppermute | solution.py:376
  19.7 2.2 %copy-start = (bf16[2048,1024]{1,0:T(8,128)(2,1)S(1)}, bf16[2048,1024]{1,0:T(8,128)(2,1)}, u32[]{:S(2)}) copy-start(bf16[2048,1024]{1,0:T(8,128)(2,1)} %refs_6_.1) | copy-start | bytes 12582916
  28.3 5.1 %collective-permute-start.10 = (bf16[64,2048]{1,0:T(8,128)(2,1)S(1)}, bf16[64,2048]{1,0:T(8,128)(2,1)S(1)}, u32[]{:S(2)}, u32[]{:S(2)}) collective-permute-start(bf16[64,2048]{1,0:T(8,128)(2,1)S(1)} %collective-permute-done.3.refs_10_), channel_id=1, source_target_pairs={{0,16},{16,0},{1,17},{17,1},{2,18},{18,2},{3,19},{19,3},{4,20},{20... | collective-permute-start | bytes 786440 | tf_op jit(solution)/shard_map/ppermute | solution.py:376
  28.7 4.7 %collective-permute-start.9 = (bf16[64,2048]{1,0:T(8,128)(2,1)S(1)}, bf16[64,2048]{1,0:T(8,128)(2,1)S(1)}, u32[]{:S(2)}, u32[]{:S(2)}) collective-permute-start(bf16[64,2048]{1,0:T(8,128)(2,1)S(1)} %collective-permute-done.2.refs_9_), channel_id=1, source_target_pairs={{0,16},{16,0},{1,17},{17,1},{2,18},{18,2},{3,19},{19,3},{4,20},{20... | collective-permute-start | bytes 786440 | tf_op jit(solution)/shard_map/ppermute | solution.py:376
  28.8 15.0 %collective-permute-start.6 = (bf16[64,2048]{1,0:T(8,128)(2,1)S(1)}, bf16[64,2048]{1,0:T(8,128)(2,1)}, u32[]{:S(2)}, u32[]{:S(2)}) collective-permute-start(bf16[64,2048]{1,0:T(8,128)(2,1)S(1)} %collective-permute-done.refs_11_), channel_id=1, source_target_pairs={{0,96},{32,0},{64,32},{96,64},{1,97},{33,1},{65,33},{97,65},{2,98}... | collective-permute-start | bytes 786440 | tf_op jit(solution)/shard_map/ppermute | solution.py:376
  32.5 11.4 %collective-permute-start.5 = (bf16[64,2048]{1,0:T(8,128)(2,1)S(1)}, bf16[64,2048]{1,0:T(8,128)(2,1)}, u32[]{:S(2)}, u32[]{:S(2)}) collective-permute-start(bf16[64,2048]{1,0:T(8,128)(2,1)S(1)} %collective-permute-done.refs_11_), channel_id=1, source_target_pairs={{0,64},{32,96},{64,0},{96,32},{1,65},{33,97},{65,1},{97,33},{2,66}... | collective-permute-start | bytes 786440 | tf_op jit(solution)/shard_map/ppermute | solution.py:376
  32.6 15.0 %collective-permute-start.4 = (bf16[64,2048]{1,0:T(8,128)(2,1)S(1)}, bf16[64,2048]{1,0:T(8,128)(2,1)}, u32[]{:S(2)}, u32[]{:S(2)}) collective-permute-start(bf16[64,2048]{1,0:T(8,128)(2,1)S(1)} %collective-permute-done.refs_11_), channel_id=1, source_target_pairs={{0,32},{32,64},{64,96},{96,0},{1,33},{33,65},{65,97},{97,1},{2,34}... | collective-permute-start | bytes 786440 | tf_op jit(solution)/shard_map/ppermute | solution.py:376
  33.4 14.2 %collective-permute-start.11 = (bf16[64,2048]{1,0:T(8,128)(2,1)S(1)}, bf16[64,2048]{1,0:T(8,128)(2,1)}, u32[]{:S(2)}, u32[]{:S(2)}) collective-permute-start(bf16[64,2048]{1,0:T(8,128)(2,1)S(1)} %collective-permute-done.refs_11_), channel_id=1, source_target_pairs={{0,16},{16,0},{1,17},{17,1},{2,18},{18,2},{3,19},{19,3},{4,20},{20... | collective-permute-start | bytes 786440 | tf_op jit(solution)/shard_map/ppermute | solution.py:376
  34.1 13.5 %collective-permute-start.8 = (bf16[64,2048]{1,0:T(8,128)(2,1)S(1)}, bf16[64,2048]{1,0:T(8,128)(2,1)}, u32[]{:S(2)}, u32[]{:S(2)}) collective-permute-start(bf16[64,2048]{1,0:T(8,128)(2,1)S(1)} %collective-permute-done.1.refs_8_), channel_id=1, source_target_pairs={{0,16},{16,0},{1,17},{17,1},{2,18},{18,2},{3,19},{19,3},{4,20},{20... | collective-permute-start | bytes 786440 | tf_op jit(solution)/shard_map/ppermute | solution.py:376
  43.9 3.8 %collective-permute-start.14 = (bf16[64,2048]{1,0:T(8,128)(2,1)}, bf16[64,2048]{1,0:T(8,128)(2,1)}, u32[]{:S(2)}, u32[]{:S(2)}) collective-permute-start(bf16[64,2048]{1,0:T(8,128)(2,1)} %collective-permute-done.6.refs_14_), channel_id=1, source_target_pairs={{0,16},{16,0},{1,17},{17,1},{2,18},{18,2},{3,19},{19,3},{4,20},{20... | collective-permute-start | bytes 786440 | tf_op jit(solution)/shard_map/ppermute | solution.py:376
  43.9 3.8 %collective-permute-start.13 = (bf16[64,2048]{1,0:T(8,128)(2,1)}, bf16[64,2048]{1,0:T(8,128)(2,1)}, u32[]{:S(2)}, u32[]{:S(2)}) collective-permute-start(bf16[64,2048]{1,0:T(8,128)(2,1)} %collective-permute-done.5.refs_13_), channel_id=1, source_target_pairs={{0,16},{16,0},{1,17},{17,1},{2,18},{18,2},{3,19},{19,3},{4,20},{20... | collective-permute-start | bytes 786440 | tf_op jit(solution)/shard_map/ppermute | solution.py:376
  47.6 1.9 %collective-permute-start.12 = (bf16[64,2048]{1,0:T(8,128)(2,1)}, bf16[64,2048]{1,0:T(8,128)(2,1)}, u32[]{:S(2)}, u32[]{:S(2)}) collective-permute-start(bf16[64,2048]{1,0:T(8,128)(2,1)} %collective-permute-done.4.refs_12_), channel_id=1, source_target_pairs={{0,16},{16,0},{1,17},{17,1},{2,18},{18,2},{3,19},{19,3},{4,20},{20... | collective-permute-start | bytes 786440 | tf_op jit(solution)/shard_map/ppermute | solution.py:376
  47.6 33.2 %copy-start.3 = (f32[1024]{0:T(1024)S(1)}, f32[1024]{0:T(1024)}, u32[]{:S(2)}) copy-start(f32[1024]{0:T(1024)} %param.15) | copy-start | bytes 12292
  53.4 27.5 %copy-start.2 = (bf16[64,2048]{1,0:T(8,128)(2,1)S(1)}, bf16[64,2048]{1,0:T(8,128)(2,1)}, u32[]{:S(2)}) copy-start(bf16[64,2048]{1,0:T(8,128)(2,1)} %copy-done.1) | copy-start | bytes 786436
  53.4 27.5 %copy-start.5 = (bf16[3,128,1024]{2,1,0:T(8,128)(2,1)S(1)}, bf16[3,128,1024]{2,1,0:T(8,128)(2,1)}, u32[]{:S(2)}) copy-start(bf16[3,128,1024]{2,1,0:T(8,128)(2,1)} %copy-done.4) | copy-start | bytes 2359300
  99.8 4.2 %collective-permute-start.15 = (bf16[8,64,2048]{2,1,0:T(8,128)(2,1)S(1)}, bf16[8,64,2048]{2,1,0:T(8,128)(2,1)S(1)}, u32[]{:S(2)}, u32[]{:S(2)}) collective-permute-start(bf16[8,64,2048]{2,1,0:T(8,128)(2,1)S(1)} %get-tuple-element.53), channel_id=1, source_target_pairs={{0,16},{16,0},{1,17},{17,1},{2,18},{18,2},{3,19},{19,3},{4,20},{20... | collective-permute-start | bytes 6291464 | tf_op jit(solution)/shard_map/ppermute | solution.py:376
  (2 other events, 1.6 us)
